TPU v7x, 128 devices: a whole 4x4x4 slice. The times are simulated.
128 devices in a mesh: dp: 128 (over z, y, x, core).
Axes of the slice: x: 4, y: 4, z: 4, core: 2. Of those that a mesh axis runs over, the one named last changes fastest.
Arguments:
- hidden: bfloat16 [131072, 5120], P('dp'), may hold values from -24 to 24
- norm_gain: float32 [5120], replicated, may hold values from 0.25 to 4
- q_cotangent: bfloat16 [131072, 128], P('dp'), may hold values from -0.015625 to 0.015625
- head_output: bfloat16 [131072, 128], P('dp'), may hold values from -6 to 6
- out_cotangent: bfloat16 [131072, 5120], P('dp'), may hold values from -0.0625 to 0.0625
- master_q: float32 [5120, 128], P('dp'), may hold values from -0.125 to 0.125
- moment_q: float32 [5120, 128], P('dp'), may hold values from -6 to 6
- second_q: float32 [5120, 128], P('dp'), may hold values from 0.01 to 0.5
- master_o: float32 [128, 5120], P(None, 'dp'), may hold values from -0.0234375 to 0.0234375
- moment_o: float32 [128, 5120], P(None, 'dp'), may hold values from -6 to 6
- second_o: float32 [128, 5120], P(None, 'dp'), may hold values from 0.01 to 0.5
Outputs:
- q_param: bfloat16 [5120, 128], replicated
- o_param: bfloat16 [128, 5120], replicated
- master_q_new: float32 [5120, 128], P('dp')
- moment_q_new: float32 [5120, 128], P('dp')
- second_q_new: float32 [5120, 128], P('dp')
- master_o_new: float32 [128, 5120], P(None, 'dp')
- moment_o_new: float32 [128, 5120], P(None, 'dp')
- second_o_new: float32 [128, 5120], P(None, 'dp')
- grad_rms: float32 [], replicated
All inputs are finite; a program needn't handle non-finite values.
Results may differ from a plain program's by a relative error of at most 0.0026.
Values may be sent and summed in bfloat16 or wider, within the bound.
A program may use at most 128 MiB of HBM per device.

v0:
```python
import jax
import jax.numpy as jnp
from jax import lax
from jax.sharding import Mesh
from jax.sharding import PartitionSpec as P

D = 5120
WIDTH = 128
STEP = 20
DP = ("dp_0", "dp_1", "dp_2", "dp_3")


norm_eps = 1e-05
beta_one = 0.9
beta_two = 0.95
learn_rate = 0.001
decay_rate = 0.1
adam_eps = 1e-08
clip_rms = 1.0


def cut_along(shard, dim, length):
    shape = shard.shape
    pieces = shard.reshape(*shape[:dim], length, shape[dim] // length, *shape[dim + 1 :])
    return jnp.moveaxis(pieces, dim, 0)


def scatter_pairs(shard, chips, core, dim):
    sizes = (lax.axis_size(chips), lax.axis_size(core))
    pieces = cut_along(shard, dim, sizes[0] * sizes[1])
    inside = pieces.shape[1:]
    pieces = pieces.reshape(*sizes, *inside).swapaxes(0, 1).reshape(-1, *inside)
    pieces = lax.psum_scatter(pieces, core, scatter_dimension=0, tiled=True)
    return lax.psum_scatter(pieces, chips, scatter_dimension=0, tiled=True)[0]


def by_axis(shard, axes):
    for axis in axes:
        shard = lax.psum(shard, axis)
    return shard


def in_one_piece(arrays, axis, dim, along):
    ends, at = ([], 0)
    for a in arrays[:-1]:
        at += a.shape[along]
        ends.append(at)
    both = jnp.concatenate(arrays, axis=along)
    return tuple(jnp.split(lax.all_gather(both, axis, axis=dim, tiled=True), ends, axis=along))


def normalize(hidden_block, norm_gain):
    hidden_wide = hidden_block.astype(jnp.float32)
    inverse = lax.rsqrt(jnp.mean(hidden_wide * hidden_wide, axis=1, keepdims=True) + norm_eps)
    return (hidden_wide * inverse * norm_gain[None, :]).astype(jnp.bfloat16)


def adamw(master, moment, second, gradient, factor):
    clipped = gradient * factor
    moment_new = beta_one * moment + (1.0 - beta_one) * clipped
    second_new = beta_two * second + (1.0 - beta_two) * clipped * clipped
    first_fix = 1.0 - beta_one**STEP
    second_fix = 1.0 - beta_two**STEP
    update = moment_new / first_fix / (jnp.sqrt(second_new / second_fix) + adam_eps)
    master_new = master - learn_rate * (update + decay_rate * master)
    return (master_new, moment_new, second_new)


def shards(
    hidden,
    norm_gain,
    q_cotangent,
    head_output,
    out_cotangent,
    master_q,
    moment_q,
    second_q,
    master_o,
    moment_o,
    second_o,
):
    normed = normalize(hidden, norm_gain)
    joined = scatter_pairs(
        jnp.concatenate(
            [
                jnp.dot(normed.T, q_cotangent, preferred_element_type=jnp.float32),
                jnp.dot(out_cotangent.T, head_output, preferred_element_type=jnp.float32),
            ],
            axis=1,
        ),
        ("dp_0", "dp_1", "dp_2"),
        "dp_3",
        0,
    )
    grad_query = joined[:, :WIDTH]
    grad_turned = joined[:, WIDTH:]
    grad_outer = grad_turned.T
    local_square = jnp.sum(grad_query * grad_query) + jnp.sum(grad_outer * grad_outer)
    total_square = by_axis(local_square, DP)
    grad_rms = jnp.sqrt(total_square / (2.0 * D * WIDTH))
    factor = jnp.minimum(1.0, clip_rms / grad_rms)
    master_q_new, moment_q_new, second_q_new = adamw(
        master_q, moment_q, second_q, grad_query, factor
    )
    master_o_new, moment_o_new, second_o_new = adamw(
        master_o, moment_o, second_o, grad_outer, factor
    )
    query_half = master_q_new.astype(jnp.bfloat16)
    outer_half = master_o_new.astype(jnp.bfloat16)
    q_param, outer_turned = in_one_piece((query_half, outer_half.T), DP, 0, 1)
    o_param = outer_turned.T
    return (
        q_param,
        o_param,
        master_q_new,
        moment_q_new,
        second_q_new,
        master_o_new,
        moment_o_new,
        second_o_new,
        grad_rms,
    )


def solution(mesh):
    split = Mesh(mesh.devices.reshape(4, 4, 4, 2), ("dp_0", "dp_1", "dp_2", "dp_3"))
    placed = (
        P(DP, None),
        P(),
        P(DP, None),
        P(DP, None),
        P(DP, None),
        P(DP, None),
        P(DP, None),
        P(DP, None),
        P(None, DP),
        P(None, DP),
        P(None, DP),
    )
    return jax.shard_map(
        shards,
        mesh=split,
        in_specs=placed,
        out_specs=(
            P(),
            P(),
            P(DP, None),
            P(DP, None),
            P(DP, None),
            P(None, DP),
            P(None, DP),
            P(None, DP),
            P(),
        ),
        check_vma=False,
    )
```

profile of v0, /device:TPU:1, one launch (start us, length us, event | category | flops | bytes accessed | tf_op | source)
XLA Modules:
  0.0 528.0 jit_solution(14018020216266289304)
XLA Ops:
  7.2 0.0 copy-start
  7.2 0.0 reduce-scatter.3.cloned.1.call-start
  7.2 0.0 copy-start.1
  7.2 6.2 %fusion = f32[1024]{0:T(1024)S(1)} fusion(bf16[1024,5120]{1,0:T(8,128)(2,1)} %param.11), kind=kLoop, calls=%fused_computation.2 | loop fusion | flops 15727616 | bytes 10489856 | tf_op jit(solution)/shard_map/reduce_sum | solution.py:54
  13.5 0.0 copy-done
  13.5 0.7 copy-done.1
  14.2 0.0 copy-start.2
  14.2 0.0 copy-start.9
  14.2 0.0 copy-start.10
  14.2 1.7 fusion.14
  15.9 2.3 copy-done.2
  18.2 0.1 copy-done.9
  18.3 0.0 copy-done.10
  18.3 3.4 fusion.3
  21.7 2.9 pad_maximum_fusion
  24.6 5.9 %copy.24 = f32[5120,256]{1,0:T(8,128)} copy(f32[5120,256]{0,1:T(8,128)} %pad_maximum_fusion) | data formatting | bytes 10485760 | tf_op jit(solution)/shard_map/concatenate | solution.py:84
  30.5 5.3 copy.25
  35.7 0.0 copy-start.3
  35.7 0.0 copy-start.4
  35.7 0.0 copy-start.5
  35.7 0.0 copy-start.6
  35.7 0.0 copy-start.7
  35.8 0.0 copy-start.8
  35.8 0.0 reduce-scatter.3.cloned.1.call-update
  35.8 0.0 reduce-scatter.5.cloned.1.call-start
  35.8 19.4 %reduce-scatter.3.cloned.1.call-done = f32[64,40,256]{2,1,0:T(8,128)} async-done(((f32[128,40,256]{2,1,0:T(8,128)}), f32[64,40,256]{2,1,0:T(8,128)}) %reduce-scatter.3.cloned.1.call-update) | async-done | bytes 2621456 | tf_op jit(solution)/shard_map/reduce_scatter | solution.py:33
  55.2 0.0 reduce-scatter.5.cloned.1.call-update
  55.2 0.0 all-gather.2.cloned.1.call-start
  55.3 311.2 %reduce-scatter.5.cloned.1.call-done = f32[1,40,256]{2,1,0:T(8,128)} async-done(((f32[64,40,256]{2,1,0:T(8,128)}), f32[1,40,256]{2,1,0:T(8,128)}) %reduce-scatter.5.cloned.1.call-update) | async-done | bytes 40976 | tf_op jit(solution)/shard_map/reduce_scatter | solution.py:34
  366.5 1.4 multiply_reduce_fusion
  369.1 6.7 %psum.28 = f32[]{:T(128)} all-reduce(f32[]{:T(128)S(6)} %add.58), channel_id=1, replica_groups=mesh['dp_0'=4,'dp_1'=4,'dp_2'=4,'dp_3'=2] {'dp_0'}, use_global_device_ids=true, to_apply=%region_5.0 | all-reduce | flops 1 | bytes 8 | tf_op jit(solution)/shard_map/psum | solution.py:39
  375.8 7.0 %psum.29 = f32[]{:T(128)} all-reduce(f32[]{:T(128)} %psum.28), channel_id=1, replica_groups=mesh['dp_0'=4,'dp_1'=4,'dp_2'=4,'dp_3'=2] {'dp_1'}, use_global_device_ids=true, to_apply=%region_6.0 | all-reduce | flops 1 | bytes 8 | tf_op jit(solution)/shard_map/psum | solution.py:39
  382.8 8.6 %psum.30 = f32[]{:T(128)} all-reduce(f32[]{:T(128)} %psum.29), channel_id=1, replica_groups=mesh['dp_0'=4,'dp_1'=4,'dp_2'=4,'dp_3'=2] {'dp_2'}, use_global_device_ids=true, to_apply=%region_7.0 | all-reduce | flops 1 | bytes 8 | tf_op jit(solution)/shard_map/psum | solution.py:39
  391.4 58.4 %psum.31 = f32[]{:T(128)} all-reduce(f32[]{:T(128)} %psum.30), channel_id=1, replica_groups=mesh['dp_0'=4,'dp_1'=4,'dp_2'=4,'dp_3'=2] {'dp_3'}, use_global_device_ids=true, to_apply=%region_8.0 | all-reduce | flops 1 | bytes 8 | tf_op jit(solution)/shard_map/psum | solution.py:39
  450.6 0.0 copy-done.3
  450.6 0.0 copy-done.4
  450.6 0.0 copy-done.5
  450.6 1.4 convert_bitcast_fusion
  452.0 0.0 copy-done.6
  452.0 0.0 copy-done.7
  452.0 0.0 copy-done.8
  452.0 1.4 fusion.10
  453.3 0.6 pad_maximum_fusion.1
  453.9 0.0 all-gather.2.cloned.1.call-update
  454.0 62.0 %all-gather.2.cloned.1.call-done = bf16[5120,256]{1,0:T(8,128)(2,1)} async-done(((bf16[40,256]{1,0:T(8,128)(2,1)}), bf16[5120,256]{1,0:T(8,128)(2,1)}) %all-gather.2.cloned.1.call-update) | async-done | bytes 2621456 | tf_op jit(solution)/shard_map/all_gather | solution.py:49
  516.0 2.9 slice_bitcast_fusion
  518.9 1.4 copy.26
  (1 shorter events, 0.0 us)
Async XLA Ops:
  7.2 6.3 %copy-start = (bf16[1024,128]{1,0:T(8,128)(2,1)S(1)}, bf16[1024,128]{1,0:T(8,128)(2,1)}, u32[]{:S(2)}) copy-start(bf16[1024,128]{1,0:T(8,128)(2,1)} %param.14) | copy-start | bytes 786436
  7.2 48.0 %reduce-scatter.3.cloned.1.call-start = ((), (), s32[]{:S(2)}) async-start(), calls=%async_computation.2 | async-start | bytes 7864320 | tf_op jit(solution)/shard_map/reduce_scatter | solution.py:33
  7.2 7.0 %copy-start.1 = (bf16[1024,5120]{1,0:T(8,128)(2,1)S(1)}, bf16[1024,5120]{1,0:T(8,128)(2,1)}, u32[]{:S(2)}) copy-start(bf16[1024,5120]{1,0:T(8,128)(2,1)} %param.15) | copy-start | bytes 31457284
  14.2 4.0 copy-start.2
  14.2 4.1 copy-start.9
  14.2 4.1 copy-start.10
  35.7 414.8 %copy-start.3 = (f32[128,40]{0,1:T(8,128)S(1)}, f32[128,40]{0,1:T(8,128)}, u32[]{:S(2)}) copy-start(f32[128,40]{0,1:T(8,128)} %param.19) | copy-start | bytes 61444
  35.7 414.8 %copy-start.4 = (f32[128,40]{0,1:T(8,128)S(1)}, f32[128,40]{0,1:T(8,128)}, u32[]{:S(2)}) copy-start(f32[128,40]{0,1:T(8,128)} %param.20) | copy-start | bytes 61444
  35.7 414.8 %copy-start.5 = (f32[128,40]{0,1:T(8,128)S(1)}, f32[128,40]{0,1:T(8,128)}, u32[]{:S(2)}) copy-start(f32[128,40]{0,1:T(8,128)} %param.21) | copy-start | bytes 61444
  35.7 416.2 %copy-start.6 = (f32[40,128]{1,0:T(8,128)S(1)}, f32[40,128]{1,0:T(8,128)}, u32[]{:S(2)}) copy-start(f32[40,128]{1,0:T(8,128)} %param.16) | copy-start | bytes 61444
  35.7 416.2 %copy-start.7 = (f32[40,128]{1,0:T(8,128)S(1)}, f32[40,128]{1,0:T(8,128)}, u32[]{:S(2)}) copy-start(f32[40,128]{1,0:T(8,128)} %param.17) | copy-start | bytes 61444
  35.8 416.2 %copy-start.8 = (f32[40,128]{1,0:T(8,128)S(1)}, f32[40,128]{1,0:T(8,128)}, u32[]{:S(2)}) copy-start(f32[40,128]{1,0:T(8,128)} %param.18) | copy-start | bytes 61444
  35.8 330.7 %reduce-scatter.5.cloned.1.call-start = ((), (), s32[]{:S(2)}) async-start(), calls=%async_computation.3 | async-start | bytes 2662400 | tf_op jit(solution)/shard_map/reduce_scatter | solution.py:34
  55.2 460.8 %all-gather.2.cloned.1.call-start = ((), (), s32[]{:S(2)}) async-start(), calls=%async_computation.4 | async-start | bytes 2641920 | tf_op jit(solution)/shard_map/all_gather | solution.py:49
Sparse Core Ops, SparseCore 0:
  35.9 19.2 reduce-scatter.2
  57.6 308.8 reduce-scatter.4
  454.1 61.8 all-gather.1
where the time goes:
time: 529 us; the launch traced here: 528 us
  waiting for transfers between devices  393 us (74%)
  blocking collectives  80.7 us (15%)
  local copies, waits for them, and re-layouts  18.7 us (4%)
  between operations  17 us (3%)
  other arithmetic  13.8 us (3%)
    reduce_scatter x1, waiting for transfers between devices, scatter_pairs(): return lax.psum_scatter(pieces, chips, scatter_dimension=0, tiled=True)[0]  311 us
    psum x4, blocking collectives, by_axis(): shard = lax.psum(shard, axis)  80.7 us
    all_gather x1, waiting for transfers between devices, in_one_piece(): lax.all_gather(both, axis, axis=dim, tiled=True)  62 us
    reduce_scatter x1, waiting for transfers between devices, scatter_pairs(): pieces = lax.psum_scatter(pieces, core, scatter_dimension=0, tiled=True)  19.4 us
  transfers between devices with their start and end apart: 3, of which 3 were waited for; matrix products, arithmetic and copies ran while one was open for 0% of the time, Pallas kernels for 0%

commit v1 on v0

v1 whole, which is shorter than its diff:
```python
import functools
import math

import jax
import jax.numpy as jnp
from jax import lax
from jax.experimental import pallas as pl
from jax.experimental.pallas import tpu as pltpu
from jax.sharding import Mesh
from jax.sharding import PartitionSpec as P

D = 5120
WIDTH = 128
STEP = 20
TOK = 1024
DP = ("z", "y", "x", "c")

norm_eps = 1e-05
beta_one = 0.9
beta_two = 0.95
learn_rate = 0.001
decay_rate = 0.1
adam_eps = 1e-08
clip_rms = 1.0

F32 = jnp.float32
BF16 = jnp.bfloat16
MESH = pl.DeviceIdType.MESH

Q_CUT = ((0, 2), (2, 4), (4, 5))
O_CUT = ((0, 1), (1, 3), (3, 5))
TILES = tuple(q[1] - q[0] + o[1] - o[0] for q, o in zip(Q_CUT, O_CUT))
ORDER = (("x", "y", "z"), ("y", "z", "x"), ("z", "x", "y"))

CHUNK = 640
CHUNKS = D // CHUNK
CHUNK_DEVS = CHUNK // 40
BLOCK = 128
BLOCKS = TOK // BLOCK


def put_chunk(grad, outs, cuts, after, j):
    tiles = grad.T.reshape(CHUNK_DEVS, 5, 8, WIDTH).astype(BF16)
    for k in range(3):
        lo, hi = cuts[k]
        at = TILES[k] - (hi - lo) if after else 0
        outs[k][pl.ds(j * CHUNK_DEVS, CHUNK_DEVS), at : at + hi - lo] = tiles[:, lo:hi]


def local_kernel(hidden, gain, qc, ho, oc, g_a, g_b, g_c, hbuf, obuf, qct, hot, squares, inverse, hsem, osem):
    outs = (g_a, g_b, g_c)

    def ocopy(j):
        cols = slice(j * CHUNK, (j + 1) * CHUNK)
        return pltpu.make_async_copy(oc.at[:, cols], obuf.at[:, cols], osem.at[j])

    def hcopy(b):
        rows = slice(b * BLOCK, (b + 1) * BLOCK)
        return pltpu.make_async_copy(hidden.at[rows], hbuf.at[rows], hsem.at[b])

    for j in range(CHUNKS):
        ocopy(j).start()
    for b in range(BLOCKS):
        hcopy(b).start()
    hot[...] = ho[...].astype(F32).T.astype(BF16)
    qct[...] = qc[...].astype(F32).T.astype(BF16)
    for j in range(CHUNKS):
        ocopy(j).wait()
        grad = jnp.dot(hot[...], obuf[:, j * CHUNK : (j + 1) * CHUNK], preferred_element_type=F32)
        put_chunk(grad, outs, O_CUT, True, j)
    for b in range(BLOCKS):
        hcopy(b).wait()

        def sum_rows(r, _):
            rows = pl.ds(pl.multiple_of(b * BLOCK + r * 16, 16), 16)
            acc = [jnp.zeros((16, 128), F32) for _ in range(4)]
            for t in range(40):
                wide = hbuf[rows, t * 128 : (t + 1) * 128].astype(F32)
                acc[t % 4] = acc[t % 4] + wide * wide
            squares[rows, :] = (acc[0] + acc[1]) + (acc[2] + acc[3])
            return 0

        lax.fori_loop(0, BLOCK // 16, sum_rows, 0)
        block = slice(b * BLOCK, (b + 1) * BLOCK)
        mean = jnp.sum(squares[block, :], axis=1, keepdims=True) * (1.0 / D)
        inverse[block, :] = jnp.broadcast_to(lax.rsqrt(mean + norm_eps), (BLOCK, 128))

        def scale_rows(r, _):
            rows = pl.ds(pl.multiple_of(b * BLOCK + r * 16, 16), 16)
            inv = inverse[rows, :]
            for t in range(40):
                cols = slice(t * 128, (t + 1) * 128)
                wide = hbuf[rows, cols].astype(F32)
                hbuf[rows, cols] = (wide * inv * gain[:, cols]).astype(BF16)
            return 0

        lax.fori_loop(0, BLOCK // 16, scale_rows, 0)
    for j in range(CHUNKS):
        grad = jnp.dot(qct[...], hbuf[:, j * CHUNK : (j + 1) * CHUNK], preferred_element_type=F32)
        put_chunk(grad, outs, Q_CUT, False, j)


def local_grads(hidden, gain, qc, ho, oc):
    vmem = pl.BlockSpec(memory_space=pltpu.VMEM)
    hbm = pl.BlockSpec(memory_space=pl.ANY)
    return pl.pallas_call(
        local_kernel,
        out_shape=[jax.ShapeDtypeStruct((128, t, 8, 128), BF16) for t in TILES],
        in_specs=[hbm, vmem, vmem, vmem, hbm],
        out_specs=[vmem] * 3,
        scratch_shapes=[
            pltpu.VMEM((TOK, D), BF16),
            pltpu.VMEM((TOK, D), BF16),
            pltpu.VMEM((128, TOK), BF16),
            pltpu.VMEM((128, TOK), BF16),
            pltpu.VMEM((TOK, 128), F32),
            pltpu.VMEM((TOK, 128), F32),
            pltpu.SemaphoreType.DMA((BLOCKS,)),
            pltpu.SemaphoreType.DMA((CHUNKS,)),
        ],
        compiler_params=pltpu.CompilerParams(vmem_limit_bytes=48 * 1024 * 1024),
        cost_estimate=pl.CostEstimate(flops=4 * TOK * D * 128, bytes_accessed=4 * TOK * D, transcendentals=0),
        name="local_grads",
    )(hidden, gain, qc, ho, oc)


def adamw(master, moment, second, gradient, factor):
    clipped = gradient * factor
    moment_new = beta_one * moment + (1.0 - beta_one) * clipped
    second_new = beta_two * second + (1.0 - beta_two) * clipped * clipped
    first_fix = 1.0 - beta_one**STEP
    second_fix = 1.0 - beta_two**STEP
    update = moment_new / first_fix / (jnp.sqrt(second_new / second_fix) + adam_eps)
    master_new = master - learn_rate * (update + decay_rate * master)
    return (master_new, moment_new, second_new)


def pick(ref, axis, index):
    return ref.at[tuple([slice(None)] * axis + [index])]


def exchange_kernel(*refs):
    g = refs[0:3]
    states = refs[3:9]
    q_out, o_out = refs[9:11]
    news = refs[11:17]
    rms_out = refs[17]
    scratch = refs[18:]
    r0, s0, r1, s1, r2, s2, r3, pp = [scratch[3 * i : 3 * i + 3] for i in range(8)]
    n0, n1, n2, n3, sem0, semr, semn0, semn, sema, sema0 = scratch[24:]

    me = {a: lax.axis_index(a) for a in DP}

    def peer(axis, j):
        size = 2 if axis == "c" else 4
        to = dict(me)
        to[axis] = lax.rem(me[axis] + j, size)
        return tuple(to[a] for a in DP)

    def remote(src, dst, sems, axis, j):
        return pltpu.make_async_remote_copy(
            src_ref=src, dst_ref=dst, send_sem=sems.at[0], recv_sem=sems.at[1],
            device_id=peer(axis, j), device_id_type=MESH,
        )

    barrier = pltpu.get_barrier_semaphore()
    pl.semaphore_signal(barrier, inc=1, device_id=peer("c", 1), device_id_type=MESH)
    for axis in "zyx":
        for j in (1, 2, 3):
            pl.semaphore_signal(barrier, inc=1, device_id=peer(axis, j), device_id_type=MESH)
    pl.semaphore_wait(barrier, 10)

    sends = []

    other = 1 - me["c"]
    first = []
    for k in range(3):
        copy = remote(g[k].at[:, :, :, other], r0[k], sem0.at[k], "c", 1)
        copy.start()
        first.append(copy)
        sends.append(copy)
    second = [[], [], []]
    for k in range(3):
        first[k].wait_recv()

        def add0(i, _, k=k):
            z, y = i // 4, lax.rem(i, 4)
            s0[k][z, y] = (g[k][z, y, :, me["c"]].astype(F32) + r0[k][z, y].astype(F32)).astype(BF16)
            return 0

        lax.fori_loop(0, 16, add0, 0)
        axis = ORDER[k][0]
        place = "zyx".index(axis)
        for j in (1, 2, 3):
            src = pick(s0[k], place, lax.rem(me[axis] + j, 4))
            copy = remote(src, r1[k].at[j - 1], semr.at[k, 0, j - 1], axis, j)
            copy.start()
            second[k].append(copy)
            sends.append(copy)
    third = [[], [], []]
    for k in range(3):
        for copy in second[k]:
            copy.wait_recv()
        axis = ORDER[k][0]
        left = "zyx".replace(axis, "")

        def add1(i, _, k=k, axis=axis):
            own = {"z": (me["z"], i), "y": (i, me["y"]), "x": (i, slice(None), me["x"])}[axis]
            total = s0[k][own].astype(F32)
            for j in range(3):
                total = total + r1[k][j, i].astype(F32)
            s1[k][i] = total.astype(BF16)
            return 0

        lax.fori_loop(0, 4, add1, 0)
        axis = ORDER[k][1]
        for j in (1, 2, 3):
            src = pick(s1[k], left.index(axis), lax.rem(me[axis] + j, 4))
            copy = remote(src, r2[k].at[j - 1], semr.at[k, 1, j - 1], axis, j)
            copy.start()
            third[k].append(copy)
            sends.append(copy)
    fourth = [[], [], []]
    for k in range(3):
        for copy in third[k]:
            copy.wait_recv()
        left = "zyx".replace(ORDER[k][0], "")
        axis = ORDER[k][1]
        own = me[axis] if left.index(axis) == 0 else (slice(None), me[axis])
        total = s1[k][own].astype(F32)
        for j in range(3):
            total = total + r2[k][j].astype(F32)
        s2[k][...] = total
        axis = ORDER[k][2]
        for j in (1, 2, 3):
            copy = remote(s2[k].at[lax.rem(me[axis] + j, 4)], r3[k].at[j - 1], semr.at[k, 2, j - 1], axis, j)
            copy.start()
            fourth[k].append(copy)
            sends.append(copy)
    grads = []
    square = jnp.zeros((8, 128), F32)
    for k in range(3):
        for copy in fourth[k]:
            copy.wait_recv()
        total = s2[k][me[ORDER[k][2]]]
        for j in range(3):
            total = total + r3[k][j]
        grads.append(total)
        square = square + jnp.sum(total * total, axis=0)

    n0[me["c"]] = square
    copy = remote(n0.at[me["c"]], n0.at[me["c"]], semn0, "c", 1)
    copy.start()
    sends.append(copy)
    copy.wait_recv()
    square = n0[0] + n0[1]
    for i, (axis, buf) in enumerate(zip("xyz", (n1, n2, n3))):
        buf[me[axis]] = square
        copies = [remote(buf.at[me[axis]], buf.at[me[axis]], semn.at[i, j - 1], axis, j) for j in (1, 2, 3)]
        for copy in copies:
            copy.start()
            sends.append(copy)
        for copy in copies:
            copy.wait_recv()
        square = (buf[0] + buf[1]) + (buf[2] + buf[3])
    total_square = jnp.sum(jnp.sum(square, axis=0, keepdims=True), axis=1, keepdims=True)
    rms = jnp.sqrt(total_square / (2.0 * D * WIDTH))
    rms_out[...] = rms
    factor = jnp.minimum(1.0, clip_rms / rms)

    here = (me["z"], me["y"], me["x"], me["c"])
    for which, cuts in enumerate((Q_CUT, O_CUT)):
        for k in range(3):
            lo, hi = cuts[k]
            at = TILES[k] - (hi - lo) if which else 0
            olds = [states[3 * which + i][lo:hi] for i in range(3)]
            fresh = adamw(*olds, grads[k][at : at + hi - lo], factor)
            for i in range(3):
                news[3 * which + i][lo:hi] = fresh[i]
            pp[k][here + (slice(at, at + hi - lo),)] = fresh[0].astype(BF16)

    waits = [None] * 3
    for step in range(3):
        for k in range(3):
            if waits[k]:
                for copy in waits[k]:
                    copy.wait_recv()
            axis = ORDER[k][2 - step]
            done = ORDER[k][3 - step :]
            index = tuple(slice(None) if a in done else me[a] for a in "zyx") + (me["c"],)
            copies = [
                remote(pp[k].at[index], pp[k].at[index], sema.at[k, step, j - 1], axis, j) for j in (1, 2, 3)
            ]
            for copy in copies:
                copy.start()
                sends.append(copy)
            waits[k] = copies
    last = []
    for k in range(3):
        for copy in waits[k]:
            copy.wait_recv()
        mine = pp[k].at[:, :, :, me["c"]]
        copy = remote(mine, mine, sema0.at[k], "c", 1)
        copy.start()
        sends.append(copy)
        last.append(copy)
    for copy in last:
        copy.wait_recv()
    for k in range(3):

        def put(i, _, k=k):
            z, y = i // 4, lax.rem(i, 4)
            whole = pp[k][z, y]
            split = Q_CUT[k][1] - Q_CUT[k][0]
            q_out[z, y, :, :, Q_CUT[k][0] : Q_CUT[k][1]] = whole[:, :, :split]
            o_out[z, y, :, :, O_CUT[k][0] : O_CUT[k][1]] = whole[:, :, split:]
            return 0

        lax.fori_loop(0, 16, put, 0)
    for copy in sends:
        copy.wait_send()


def exchange(g, states):
    vmem = pl.BlockSpec(memory_space=pltpu.VMEM)
    per = lambda lead, dtype: [pltpu.VMEM(lead + (t, 8, 128), dtype) for t in TILES]
    tile = jax.ShapeDtypeStruct((5, 8, 128), F32)
    whole = jax.ShapeDtypeStruct((4, 4, 4, 2, 5, 8, 128), BF16)
    return pl.pallas_call(
        exchange_kernel,
        out_shape=[whole, whole] + [tile] * 6 + [jax.ShapeDtypeStruct((1, 1), F32)],
        in_specs=[vmem] * 9,
        out_specs=[vmem] * 9,
        scratch_shapes=per((4, 4, 4), BF16)
        + per((4, 4, 4), BF16)
        + per((3, 4, 4), BF16)
        + per((4, 4), BF16)
        + per((3, 4), BF16)
        + per((4,), F32)
        + per((3,), F32)
        + per((4, 4, 4, 2), BF16)
        + [
            pltpu.VMEM((2, 8, 128), F32),
            pltpu.VMEM((4, 8, 128), F32),
            pltpu.VMEM((4, 8, 128), F32),
            pltpu.VMEM((4, 8, 128), F32),
            pltpu.SemaphoreType.DMA((3, 2)),
            pltpu.SemaphoreType.DMA((3, 3, 3, 2)),
            pltpu.SemaphoreType.DMA((2,)),
            pltpu.SemaphoreType.DMA((3, 3, 2)),
            pltpu.SemaphoreType.DMA((3, 3, 3, 2)),
            pltpu.SemaphoreType.DMA((3, 2)),
        ],
        compiler_params=pltpu.CompilerParams(
            collective_id=0, has_side_effects=True, vmem_limit_bytes=32 * 1024 * 1024
        ),
        name="exchange",
    )(*g, *states)


def shards(hidden, norm_gain, q_cotangent, head_output, out_cotangent, master_q, moment_q, second_q, master_o, moment_o, second_o):
    g = local_grads(hidden, norm_gain.reshape(1, D), q_cotangent, head_output, out_cotangent)
    g = [a.reshape(4, 4, 4, 2, *a.shape[1:]) for a in g]
    states = [a.reshape(5, 8, 128) for a in (master_q, moment_q, second_q, master_o.T, moment_o.T, second_o.T)]
    out = exchange(g, states)
    q_param = out[0].reshape(D, WIDTH)
    o_param = out[1].reshape(D, WIDTH).T
    fresh = [a.reshape(40, 128) for a in out[2:8]]
    return (q_param, o_param, *fresh[:3], *[a.T for a in fresh[3:]], out[8].reshape(()))


def solution(mesh):
    split = Mesh(mesh.devices.reshape(4, 4, 4, 2), DP)
    tall, wide, whole = P(DP, None), P(None, DP), P()
    return jax.shard_map(
        shards,
        mesh=split,
        in_specs=(tall, whole, tall, tall, tall, tall, tall, tall, wide, wide, wide),
        out_specs=(whole, whole, tall, tall, tall, wide, wide, wide, whole),
        check_vma=False,
    )
```

time: 529 us -> 82.8 us (0.16)
  waiting for transfers between devices: 393 us -> 0 us
  blocking collectives: 80.7 us -> 0 us
  Pallas kernels: 0 us -> 71.2 us
  between operations: 17 us -> 2.51 us
  other arithmetic: 13.8 us -> 0 us
  local copies, waits for them, and re-layouts: 18.7 us -> 8.78 us
    reduce_scatter x2 -> x0, waiting for transfers between devices: 331 us -> none  [the longest x1 311 us: scatter_pairs(): return lax.psum_scatter(pieces, chips, scatter_dimension=0, tiled=True)[0]]
    psum x4 -> x0, blocking collectives: 80.7 us -> none  [by_axis(): shard = lax.psum(shard, axis)]
    pallas_call x0 -> x2, Pallas kernels: none -> 71.2 us  [the longest x1 55.4 us: exchange(): pl.pallas_call(exchange_kernel, out_shape=[whole, whole] + [tile] * 6 + [...]
    all_gather x1 -> x0, waiting for transfers between devices: 62 us -> none  [in_one_piece(): lax.all_gather(both, axis, axis=dim, tiled=True)]
    transpose x2 -> x0, local copies, waits for them, and re-layouts: 8.19 us -> none  [the longest x1 5.25 us: scatter_pairs(): pieces = pieces.reshape(*sizes, *inside).swapaxes(0, 1).reshape(-1, *inside)]
    reduce_sum x2 -> x0, other arithmetic: 7.58 us -> none  [the longest x1 6.23 us: normalize(): jnp.mean(hidden_wide * hidden_wide, axis=1, keepdims=True) + norm_eps]
    concatenate x1 -> x0, local copies, waits for them, and re-layouts: 5.92 us -> none  [shards(): jnp.concatenate([jnp.dot(normed.T, q_cotangent, preferred_element_type=jn...]
  transfers between devices with their start and end apart: 3 -> 0, of which waited for: 3 -> 0; matrix products, arithmetic and copies ran while one was open for 0% -> 0% of each run, Pallas kernels for 0% -> 0%
where the time goes in v1:
time: 82.8 us; the launch traced here: 82.5 us
  Pallas kernels  71.2 us (86%)
  local copies, waits for them, and re-layouts  8.78 us (11%)
  between operations  2.51 us (3%)
    pallas_call x1, Pallas kernels, exchange(): pl.pallas_call(exchange_kernel, out_shape=[whole, whole] + [tile] * 6 + [...  55.4 us
    pallas_call x1, Pallas kernels, local_grads(): pl.pallas_call(local_kernel, out_shape=[jax.ShapeDtypeStruct((128, t, 8,...  15.8 us
    unnamed x25, local copies, waits for them, and re-layouts  7.33 us

profile of v1, /device:TPU:1, one launch (start us, length us, event | category | flops | bytes accessed | tf_op | source)
XLA Modules:
  0.0 82.5 jit_solution(9617860802061469243)
XLA Ops:
  0.6 0.0 copy-start
  0.7 0.9 %copy-done = bf16[1024,128]{1,0:T(8,128)(2,1)S(1)} copy-done((bf16[1024,128]{1,0:T(8,128)(2,1)S(1)}, bf16[1024,128]{1,0:T(8,128)(2,1)}, u32[]{:S(2)}) %copy-start) | copy-done | bytes 262168
  1.6 0.0 copy-start.1
  1.6 0.9 %copy-done.1 = bf16[1024,128]{1,0:T(8,128)(2,1)S(1)} copy-done((bf16[1024,128]{1,0:T(8,128)(2,1)S(1)}, bf16[1024,128]{1,0:T(8,128)(2,1)}, u32[]{:S(2)}) %copy-start.1) | copy-done | bytes 262168
  2.5 0.0 copy-start.2
  2.5 0.7 copy-done.2
  3.3 0.0 copy-start.3
  3.3 0.0 copy-start.4
  3.3 0.0 copy-start.5
  3.3 0.0 copy-start.6
  3.3 0.0 copy-start.7
  3.3 0.0 copy-start.8
  3.3 15.8 %local_grads.1 = (bf16[128,3,8,128]{3,2,1,0:T(8,128)(2,1)S(1)}, bf16[128,4,8,128]{3,2,1,0:T(8,128)(2,1)S(1)}, bf16[128,3,8,128]{3,2,1,0:T(8,128)(2,1)S(1)}) custom-call(bf16[1024,5120]{1,0:T(8,128)(2,1)} %hidden.1, f32[1,5120]{1,0:T(1,128)S(1)} %bitcast.37, bf16[1024,128]{1,0:T(8,128)(2,1)S(1)} %copy-done, bf16[1024,128]{1,0:T(8,128)(2,1)S(1)} %copy-done.1, ...), custom_call_target="tpu_custom_call" | custom-call | flops 2684354560 | bytes 20971520 | tf_op jit(solution)/shard_map/local_grads/pallas_call | solution.py:106
  19.1 0.0 copy-done.3
  19.1 0.0 copy-done.4
  19.1 0.0 copy-done.5
  19.1 0.0 copy-done.6
  19.2 0.0 copy-done.7
  19.2 0.0 copy-done.8
  19.2 55.4 %exchange.1 = (bf16[4,4,4,2,5,8,128]{6,5,4,3,2,1,0:T(8,128)(2,1)S(1)}, bf16[4,4,4,2,5,8,128]{6,5,4,3,2,1,0:T(8,128)(2,1)S(1)}, f32[5,8,128]{2,1,0:T(8,128)S(1)},...) custom-call(bf16[4,4,4,2,3,8,128]{6,5,4,3,2,1,0:T(8,128)(2,1)S(1)} %, ...), custom_call_target="tpu_custom_call" | custom-call | tf_op jit(solution)/shard_map/exchange/pallas_call | solution.py:329
  74.6 1.4 %copy.20 = bf16[5120,128]{0,1:T(8,128)(2,1)} copy(bf16[5120,128]{1,0:T(8,128)(2,1)S(1)} %bitcast.33) | data formatting | bytes 2621440 | tf_op jit(solution)/shard_map/reshape | solution.py:367
  76.1 1.1 %copy.29 = bf16[5120,128]{1,0:T(8,128)(2,1)} copy(bf16[5120,128]{1,0:T(8,128)(2,1)S(1)} %bitcast.32) | data formatting | bytes 2621440
  77.1 0.6 copy.30
  77.7 0.6 copy.31
  78.3 0.6 copy.32
  78.9 0.6 copy.33
  79.6 0.6 copy.34
  80.2 0.6 copy.35
Async XLA Ops:
  0.6 1.0 %copy-start = (bf16[1024,128]{1,0:T(8,128)(2,1)S(1)}, bf16[1024,128]{1,0:T(8,128)(2,1)}, u32[]{:S(2)}) copy-start(bf16[1024,128]{1,0:T(8,128)(2,1)} %qc.1) | copy-start | bytes 786436
  1.6 0.9 %copy-start.1 = (bf16[1024,128]{1,0:T(8,128)(2,1)S(1)}, bf16[1024,128]{1,0:T(8,128)(2,1)}, u32[]{:S(2)}) copy-start(bf16[1024,128]{1,0:T(8,128)(2,1)} %ho.1) | copy-start | bytes 786436
  2.5 0.7 copy-start.2
  3.3 15.8 %copy-start.3 = (f32[40,128]{1,0:T(8,128)S(1)}, f32[40,128]{1,0:T(8,128)}, u32[]{:S(2)}) copy-start(f32[40,128]{1,0:T(8,128)} %param.16) | copy-start | bytes 61444
  3.3 15.8 %copy-start.4 = (f32[40,128]{1,0:T(8,128)S(1)}, f32[40,128]{1,0:T(8,128)}, u32[]{:S(2)}) copy-start(f32[40,128]{1,0:T(8,128)} %param.17) | copy-start | bytes 61444
  3.3 15.9 %copy-start.5 = (f32[40,128]{1,0:T(8,128)S(1)}, f32[40,128]{1,0:T(8,128)}, u32[]{:S(2)}) copy-start(f32[40,128]{1,0:T(8,128)} %param.18) | copy-start | bytes 61444
  3.3 15.9 %copy-start.6 = (f32[128,40]{0,1:T(8,128)S(1)}, f32[128,40]{0,1:T(8,128)}, u32[]{:S(2)}) copy-start(f32[128,40]{0,1:T(8,128)} %param.19) | copy-start | bytes 61444
  3.3 15.9 %copy-start.7 = (f32[128,40]{0,1:T(8,128)S(1)}, f32[128,40]{0,1:T(8,128)}, u32[]{:S(2)}) copy-start(f32[128,40]{0,1:T(8,128)} %param.20) | copy-start | bytes 61444
  3.3 15.9 %copy-start.8 = (f32[128,40]{0,1:T(8,128)S(1)}, f32[128,40]{0,1:T(8,128)}, u32[]{:S(2)}) copy-start(f32[128,40]{0,1:T(8,128)} %param.21) | copy-start | bytes 61444

commit v2 on v1

--- a/solution.py
+++ b/solution.py
@@ -47,8 +47,11 @@
         outs[k][pl.ds(j * CHUNK_DEVS, CHUNK_DEVS), at : at + hi - lo] = tiles[:, lo:hi]
 
 
-def local_kernel(hidden, gain, qc, ho, oc, g_a, g_b, g_c, hbuf, obuf, qct, hot, squares, inverse, hsem, osem):
+def local_kernel(hidden, gain_hbm, qc_hbm, ho_hbm, oc, g_a, g_b, g_c, hbuf, obuf, gain, qc, ho, qct, hot, squares, inverse, hsem, osem, ssem):
     outs = (g_a, g_b, g_c)
+    small = [pltpu.make_async_copy(a, b, ssem.at[i]) for i, (a, b) in enumerate(((ho_hbm, ho), (qc_hbm, qc), (gain_hbm, gain)))]
+    for copy in small:
+        copy.start()
 
     def ocopy(j):
         cols = slice(j * CHUNK, (j + 1) * CHUNK)
@@ -62,6 +65,8 @@
         ocopy(j).start()
     for b in range(BLOCKS):
         hcopy(b).start()
+    for copy in small:
+        copy.wait()
     hot[...] = ho[...].astype(F32).T.astype(BF16)
     qct[...] = qc[...].astype(F32).T.astype(BF16)
     for j in range(CHUNKS):
@@ -102,21 +107,25 @@
 
 def local_grads(hidden, gain, qc, ho, oc):
     vmem = pl.BlockSpec(memory_space=pltpu.VMEM)
-    hbm = pl.BlockSpec(memory_space=pl.ANY)
+    hbm = pl.BlockSpec(memory_space=pltpu.HBM)
     return pl.pallas_call(
         local_kernel,
         out_shape=[jax.ShapeDtypeStruct((128, t, 8, 128), BF16) for t in TILES],
-        in_specs=[hbm, vmem, vmem, vmem, hbm],
+        in_specs=[hbm] * 5,
         out_specs=[vmem] * 3,
         scratch_shapes=[
             pltpu.VMEM((TOK, D), BF16),
             pltpu.VMEM((TOK, D), BF16),
+            pltpu.VMEM((1, D), F32),
+            pltpu.VMEM((TOK, 128), BF16),
+            pltpu.VMEM((TOK, 128), BF16),
             pltpu.VMEM((128, TOK), BF16),
             pltpu.VMEM((128, TOK), BF16),
             pltpu.VMEM((TOK, 128), F32),
             pltpu.VMEM((TOK, 128), F32),
             pltpu.SemaphoreType.DMA((BLOCKS,)),
             pltpu.SemaphoreType.DMA((CHUNKS,)),
+            pltpu.SemaphoreType.DMA((3,)),
         ],
         compiler_params=pltpu.CompilerParams(vmem_limit_bytes=48 * 1024 * 1024),
         cost_estimate=pl.CostEstimate(flops=4 * TOK * D * 128, bytes_accessed=4 * TOK * D, transcendentals=0),
@@ -142,20 +151,19 @@
 def exchange_kernel(*refs):
     g = refs[0:3]
     states = refs[3:9]
-    q_out, o_out = refs[9:11]
-    news = refs[11:17]
-    rms_out = refs[17]
-    scratch = refs[18:]
-    r0, s0, r1, s1, r2, s2, r3, pp = [scratch[3 * i : 3 * i + 3] for i in range(8)]
-    n0, n1, n2, n3, sem0, semr, semn0, semn, sema, sema0 = scratch[24:]
+    pp = refs[9:12]
+    news, rms_out = refs[12:14]
+    scratch = refs[14:]
+    r0, s0, r1, s1, r2, s2, r3 = [scratch[3 * i : 3 * i + 3] for i in range(7)]
+    nall, sem0, semr, semn, sema, semb, semc, semd = scratch[21:]
 
     me = {a: lax.axis_index(a) for a in DP}
+    ring = {a: [me[a]] + [lax.rem(me[a] + j, 4) for j in (1, 2, 3)] for a in "zyx"}
+    ring["c"] = [me["c"], 1 - me["c"]]
+    back = {a: [me[a]] + [lax.rem(me[a] + 4 - j, 4) for j in (1, 2, 3)] for a in "zyx"}
 
     def peer(axis, j):
-        size = 2 if axis == "c" else 4
-        to = dict(me)
-        to[axis] = lax.rem(me[axis] + j, size)
-        return tuple(to[a] for a in DP)
+        return tuple(ring[a][j] if a == axis else me[a] for a in DP)
 
     def remote(src, dst, sems, axis, j):
         return pltpu.make_async_remote_copy(
@@ -163,12 +171,15 @@
             device_id=peer(axis, j), device_id_type=MESH,
         )
 
+    others = [
+        (ring["z"][dz], ring["y"][dy], ring["x"][dx], ring["c"][dc])
+        for dz in (2, 3, 1, 0) for dy in (2, 3, 1, 0) for dx in (2, 3, 1, 0) for dc in (1, 0)
+        if dz + dy + dx + dc > 0
+    ]
     barrier = pltpu.get_barrier_semaphore()
-    pl.semaphore_signal(barrier, inc=1, device_id=peer("c", 1), device_id_type=MESH)
-    for axis in "zyx":
-        for j in (1, 2, 3):
-            pl.semaphore_signal(barrier, inc=1, device_id=peer(axis, j), device_id_type=MESH)
-    pl.semaphore_wait(barrier, 10)
+    for device in others:
+        pl.semaphore_signal(barrier, inc=1, device_id=device, device_id_type=MESH)
+    pl.semaphore_wait(barrier, len(others))
 
     sends = []
 
@@ -192,7 +203,7 @@
         axis = ORDER[k][0]
         place = "zyx".index(axis)
         for j in (1, 2, 3):
-            src = pick(s0[k], place, lax.rem(me[axis] + j, 4))
+            src = pick(s0[k], place, ring[axis][j])
             copy = remote(src, r1[k].at[j - 1], semr.at[k, 0, j - 1], axis, j)
             copy.start()
             second[k].append(copy)
@@ -215,7 +226,7 @@
         lax.fori_loop(0, 4, add1, 0)
         axis = ORDER[k][1]
         for j in (1, 2, 3):
-            src = pick(s1[k], left.index(axis), lax.rem(me[axis] + j, 4))
+            src = pick(s1[k], left.index(axis), ring[axis][j])
             copy = remote(src, r2[k].at[j - 1], semr.at[k, 1, j - 1], axis, j)
             copy.start()
             third[k].append(copy)
@@ -233,7 +244,7 @@
         s2[k][...] = total
         axis = ORDER[k][2]
         for j in (1, 2, 3):
-            copy = remote(s2[k].at[lax.rem(me[axis] + j, 4)], r3[k].at[j - 1], semr.at[k, 2, j - 1], axis, j)
+            copy = remote(s2[k].at[ring[axis][j]], r3[k].at[j - 1], semr.at[k, 2, j - 1], axis, j)
             copy.start()
             fourth[k].append(copy)
             sends.append(copy)
@@ -248,75 +259,75 @@
         grads.append(total)
         square = square + jnp.sum(total * total, axis=0)
 
-    n0[me["c"]] = square
-    copy = remote(n0.at[me["c"]], n0.at[me["c"]], semn0, "c", 1)
-    copy.start()
-    sends.append(copy)
-    copy.wait_recv()
-    square = n0[0] + n0[1]
-    for i, (axis, buf) in enumerate(zip("xyz", (n1, n2, n3))):
-        buf[me[axis]] = square
-        copies = [remote(buf.at[me[axis]], buf.at[me[axis]], semn.at[i, j - 1], axis, j) for j in (1, 2, 3)]
-        for copy in copies:
-            copy.start()
-            sends.append(copy)
-        for copy in copies:
-            copy.wait_recv()
-        square = (buf[0] + buf[1]) + (buf[2] + buf[3])
+    number = ((me["z"] * 4 + me["y"]) * 4 + me["x"]) * 2 + me["c"]
+    mine = nall.at[pl.ds(number, 1)]
+    nall[pl.ds(number, 1), :] = jnp.sum(square, axis=0, keepdims=True)
+    for device in others:
+        pltpu.make_async_remote_copy(
+            src_ref=mine, dst_ref=mine, send_sem=semn.at[0], recv_sem=semn.at[1],
+            device_id=device, device_id_type=MESH,
+        ).start()
+    rest = nall.at[pl.ds(0, len(others))]
+    every = remote(rest, rest, semn, "c", 1)
+    every.wait_recv()
+    square = nall[...]
     total_square = jnp.sum(jnp.sum(square, axis=0, keepdims=True), axis=1, keepdims=True)
     rms = jnp.sqrt(total_square / (2.0 * D * WIDTH))
     rms_out[...] = rms
     factor = jnp.minimum(1.0, clip_rms / rms)
 
     here = (me["z"], me["y"], me["x"], me["c"])
-    for which, cuts in enumerate((Q_CUT, O_CUT)):
-        for k in range(3):
+    for k in range(3):
+        for which, cuts in enumerate((Q_CUT, O_CUT)):
             lo, hi = cuts[k]
             at = TILES[k] - (hi - lo) if which else 0
             olds = [states[3 * which + i][lo:hi] for i in range(3)]
             fresh = adamw(*olds, grads[k][at : at + hi - lo], factor)
             for i in range(3):
-                news[3 * which + i][lo:hi] = fresh[i]
+                news[3 * which + i, lo:hi] = fresh[i]
             pp[k][here + (slice(at, at + hi - lo),)] = fresh[0].astype(BF16)
 
-    waits = [None] * 3
-    for step in range(3):
+    def block(k, i, j, every=True):
+        one, two, three = ORDER[k]
+        index = dict(me)
+        index[one], index[two] = back[one][i], back[two][j]
+        if every:
+            index[three] = slice(None)
+        return pp[k].at[tuple(index[a] for a in DP)]
+
+    along3, along2, along1, cross = [{} for _ in range(4)]
+
+    def go(kept, key, ref, sems, axis, j):
+        kept[key] = remote(ref, ref, sems, axis, j)
+        kept[key].start()
+        sends.append(kept[key])
+
+    near = (1, 3, 2)
+    for k in range(3):
+        for j in near:
+            go(along3, (k, j), block(k, 0, 0, False), sema.at[k, j - 1], ORDER[k][2], j)
+    for k in range(3):
+        for j in near:
+            along3[k, j].wait_recv()
+        for j in near:
+            go(along2, (k, j), block(k, 0, 0), semb.at[k, j - 1], ORDER[k][1], j)
+        for j in near:
+            go(along1, (k, 0, j), block(k, 0, 0), semc.at[k, 0, j - 1], ORDER[k][0], j)
+        go(cross, (k, 0, 0), block(k, 0, 0), semd.at[k, 0, 0], "c", 1)
+    for two in near:
         for k in range(3):
-            if waits[k]:
-                for copy in waits[k]:
-                    copy.wait_recv()
-            axis = ORDER[k][2 - step]
-            done = ORDER[k][3 - step :]
-            index = tuple(slice(None) if a in done else me[a] for a in "zyx") + (me["c"],)
-            copies = [
-                remote(pp[k].at[index], pp[k].at[index], sema.at[k, step, j - 1], axis, j) for j in (1, 2, 3)
-            ]
-            for copy in copies:
-                copy.start()
-                sends.append(copy)
-            waits[k] = copies
-    last = []
-    for k in range(3):
-        for copy in waits[k]:
-            copy.wait_recv()
-        mine = pp[k].at[:, :, :, me["c"]]
-        copy = remote(mine, mine, sema0.at[k], "c", 1)
-        copy.start()
-        sends.append(copy)
-        last.append(copy)
-    for copy in last:
+            along2[k, two].wait_recv()
+            for j in near:
+                go(along1, (k, two, j), block(k, 0, two), semc.at[k, two, j - 1], ORDER[k][0], j)
+            go(cross, (k, 0, two), block(k, 0, two), semd.at[k, 0, two], "c", 1)
+    for two in (0,) + near:
+        for j in near:
+            for k in range(3):
+                along1[k, two, j].wait_recv()
+                go(cross, (k, j, two), block(k, j, two), semd.at[k, j, two], "c", 1)
+    for copy in cross.values():
         copy.wait_recv()
-    for k in range(3):
-
-        def put(i, _, k=k):
-            z, y = i // 4, lax.rem(i, 4)
-            whole = pp[k][z, y]
-            split = Q_CUT[k][1] - Q_CUT[k][0]
-            q_out[z, y, :, :, Q_CUT[k][0] : Q_CUT[k][1]] = whole[:, :, :split]
-            o_out[z, y, :, :, O_CUT[k][0] : O_CUT[k][1]] = whole[:, :, split:]
-            return 0
-
-        lax.fori_loop(0, 16, put, 0)
+    every.wait_send()
     for copy in sends:
         copy.wait_send()
 
@@ -324,13 +335,12 @@
 def exchange(g, states):
     vmem = pl.BlockSpec(memory_space=pltpu.VMEM)
     per = lambda lead, dtype: [pltpu.VMEM(lead + (t, 8, 128), dtype) for t in TILES]
-    tile = jax.ShapeDtypeStruct((5, 8, 128), F32)
-    whole = jax.ShapeDtypeStruct((4, 4, 4, 2, 5, 8, 128), BF16)
     return pl.pallas_call(
         exchange_kernel,
-        out_shape=[whole, whole] + [tile] * 6 + [jax.ShapeDtypeStruct((1, 1), F32)],
+        out_shape=[jax.ShapeDtypeStruct((4, 4, 4, 2, t, 8, 128), BF16) for t in TILES]
+        + [jax.ShapeDtypeStruct((6, 5, 8, 128), F32), jax.ShapeDtypeStruct((1, 1), F32)],
         in_specs=[vmem] * 9,
-        out_specs=[vmem] * 9,
+        out_specs=[vmem] * 5,
         scratch_shapes=per((4, 4, 4), BF16)
         + per((4, 4, 4), BF16)
         + per((3, 4, 4), BF16)
@@ -338,18 +348,15 @@
         + per((3, 4), BF16)
         + per((4,), F32)
         + per((3,), F32)
-        + per((4, 4, 4, 2), BF16)
         + [
-            pltpu.VMEM((2, 8, 128), F32),
-            pltpu.VMEM((4, 8, 128), F32),
-            pltpu.VMEM((4, 8, 128), F32),
-            pltpu.VMEM((4, 8, 128), F32),
+            pltpu.VMEM((128, 128), F32),
             pltpu.SemaphoreType.DMA((3, 2)),
             pltpu.SemaphoreType.DMA((3, 3, 3, 2)),
             pltpu.SemaphoreType.DMA((2,)),
             pltpu.SemaphoreType.DMA((3, 3, 2)),
-            pltpu.SemaphoreType.DMA((3, 3, 3, 2)),
-            pltpu.SemaphoreType.DMA((3, 2)),
+            pltpu.SemaphoreType.DMA((3, 3, 2)),
+            pltpu.SemaphoreType.DMA((3, 4, 3, 2)),
+            pltpu.SemaphoreType.DMA((3, 4, 4, 2)),
         ],
         compiler_params=pltpu.CompilerParams(
             collective_id=0, has_side_effects=True, vmem_limit_bytes=32 * 1024 * 1024
@@ -358,15 +365,75 @@
     )(*g, *states)
 
 
+GROUP = 16
+
+
+def finish_kernel(p_a, p_b, p_c, news, rms, q_out, o_out, *rest):
+    outs, rms_out = rest[:6], rest[6]
+    turned, qsem, nsem, osem = rest[7:]
+    pp = (p_a, p_b, p_c)
+    copies = []
+
+    def go(src, dst, sem):
+        copies.append(pltpu.make_async_copy(src, dst, sem))
+        copies[-1].start()
+
+    for k in range(3):
+        lo, hi = Q_CUT[k]
+        go(pp[k].at[:, 0 : hi - lo], q_out.at[:, lo:hi], qsem.at[k])
+    for i in range(6):
+        go(news.at[i], outs[i], nsem.at[i])
+    rms_out[...] = rms[...]
+    where = {}
+    for k in range(3):
+        lo, hi = O_CUT[k]
+        for t in range(lo, hi):
+            where[t] = (k, TILES[k] - hi + t)
+    for group in range(128 // GROUP):
+        for b in range(5):
+            tiles = []
+            for i in range(16):
+                flat = b * 16 + i
+                k, t = where[flat % 5]
+                tiles.append(pp[k][group * GROUP + flat // 5, t].astype(F32))
+            wide = jnp.concatenate(tiles, axis=0).T
+            at = group * 640 + b * 128
+            turned[:, at : at + 128] = wide.astype(BF16)
+        cols = slice(group * 640, (group + 1) * 640)
+        go(turned.at[:, cols], o_out.at[:, cols], osem.at[group])
+    for copy in copies:
+        copy.wait()
+
+
+def finish(pp, news, rms):
+    vmem = pl.BlockSpec(memory_space=pltpu.VMEM)
+    hbm = pl.BlockSpec(memory_space=pltpu.HBM)
+    return pl.pallas_call(
+        finish_kernel,
+        out_shape=[jax.ShapeDtypeStruct((128, 5, 8, 128), BF16), jax.ShapeDtypeStruct((WIDTH, D), BF16)]
+        + [jax.ShapeDtypeStruct((5, 8, 128), F32)] * 6
+        + [jax.ShapeDtypeStruct((1, 1), F32)],
+        in_specs=[vmem] * 5,
+        out_specs=[hbm] * 8 + [vmem],
+        scratch_shapes=[
+            pltpu.VMEM((WIDTH, D), BF16),
+            pltpu.SemaphoreType.DMA((3,)),
+            pltpu.SemaphoreType.DMA((6,)),
+            pltpu.SemaphoreType.DMA((128 // GROUP,)),
+        ],
+        compiler_params=pltpu.CompilerParams(vmem_limit_bytes=16 * 1024 * 1024),
+        name="finish",
+    )(*pp, news, rms)
+
+
 def shards(hidden, norm_gain, q_cotangent, head_output, out_cotangent, master_q, moment_q, second_q, master_o, moment_o, second_o):
     g = local_grads(hidden, norm_gain.reshape(1, D), q_cotangent, head_output, out_cotangent)
     g = [a.reshape(4, 4, 4, 2, *a.shape[1:]) for a in g]
     states = [a.reshape(5, 8, 128) for a in (master_q, moment_q, second_q, master_o.T, moment_o.T, second_o.T)]
     out = exchange(g, states)
-    q_param = out[0].reshape(D, WIDTH)
-    o_param = out[1].reshape(D, WIDTH).T
+    out = finish([a.reshape(128, *a.shape[4:]) for a in out[:3]], out[3], out[4])
     fresh = [a.reshape(40, 128) for a in out[2:8]]
-    return (q_param, o_param, *fresh[:3], *[a.T for a in fresh[3:]], out[8].reshape(()))
+    return (out[0].reshape(D, WIDTH), out[1], *fresh[:3], *[a.T for a in fresh[3:]], out[8].reshape(()))
 
 
 def solution(mesh):

time: 82.8 us -> 74.1 us (0.89)
  local copies, waits for them, and re-layouts: 8.78 us -> 2.64 us
  between operations: 2.51 us -> 0.74 us
    unnamed x25 -> x18, local copies, waits for them, and re-layouts: 7.33 us -> 2.64 us
    reshape x1 -> x0, local copies, waits for them, and re-layouts: 1.44 us -> none  [shards(): o_param = out[1].reshape(D, WIDTH).T]
    pallas_call x1 -> x2, Pallas kernels: 55.4 us -> 54.7 us  [the longest x1 51.7 us: exchange(): pl.pallas_call(exchange_kernel, out_shape=[jax.ShapeDtypeStruct((4, 4, 4,...]
where the time goes in v2:
time: 74.1 us; the launch traced here: 73.9 us
  Pallas kernels  70.5 us (95%)
  local copies, waits for them, and re-layouts  2.64 us (4%)
    pallas_call x1, Pallas kernels, exchange(): pl.pallas_call(exchange_kernel, out_shape=[jax.ShapeDtypeStruct((4, 4, 4,...  51.7 us
    pallas_call x1, Pallas kernels, local_grads(): pl.pallas_call(local_kernel, out_shape=[jax.ShapeDtypeStruct((128, t, 8,...  15.8 us
    pallas_call x1, Pallas kernels, finish(): pl.pallas_call(finish_kernel, out_shape=[jax.ShapeDtypeStruct((128, 5, 8,...  2.92 us
    unnamed x18, local copies, waits for them, and re-layouts  2.64 us

profile of v2, /device:TPU:1, one launch (start us, length us, event | category | flops | bytes accessed | tf_op | source)
XLA Modules:
  0.0 73.9 jit_solution(9177515220529381012)
XLA Ops:
  0.6 0.0 copy-start
  0.7 0.9 %copy-done = bf16[1024,128]{1,0:T(8,128)(2,1)S(1)} copy-done((bf16[1024,128]{1,0:T(8,128)(2,1)S(1)}, bf16[1024,128]{1,0:T(8,128)(2,1)}, u32[]{:S(2)}) %copy-start) | copy-done | bytes 262168
  1.6 0.0 copy-start.1
  1.6 0.9 %copy-done.1 = bf16[1024,128]{1,0:T(8,128)(2,1)S(1)} copy-done((bf16[1024,128]{1,0:T(8,128)(2,1)S(1)}, bf16[1024,128]{1,0:T(8,128)(2,1)}, u32[]{:S(2)}) %copy-start.1) | copy-done | bytes 262168
  2.5 0.0 copy-start.2
  2.5 0.7 copy-done.2
  3.3 0.0 copy-start.3
  3.3 0.0 copy-start.4
  3.3 0.0 copy-start.5
  3.3 0.0 copy-start.6
  3.3 0.0 copy-start.7
  3.3 0.0 copy-start.8
  3.3 15.8 %local_grads.1 = (bf16[128,3,8,128]{3,2,1,0:T(8,128)(2,1)S(1)}, bf16[128,4,8,128]{3,2,1,0:T(8,128)(2,1)S(1)}, bf16[128,3,8,128]{3,2,1,0:T(8,128)(2,1)S(1)}) custom-call(bf16[1024,5120]{1,0:T(8,128)(2,1)} %hidden.1, f32[1,5120]{1,0:T(1,128)S(1)} %bitcast.39, bf16[1024,128]{1,0:T(8,128)(2,1)S(1)} %copy-done, bf16[1024,128]{1,0:T(8,128)(2,1)S(1)} %copy-done.1, ...), custom_call_target="tpu_custom_call" | custom-call | flops 2684354560 | bytes 20971520 | tf_op jit(solution)/shard_map/local_grads/pallas_call | solution.py:111
  19.2 0.0 copy-done.3
  19.2 0.0 copy-done.4
  19.2 0.0 copy-done.5
  19.2 0.0 copy-done.6
  19.2 0.0 copy-done.7
  19.2 0.0 copy-done.8
  19.2 51.7 %exchange.1 = (bf16[4,4,4,2,3,8,128]{6,5,4,3,2,1,0:T(8,128)(2,1)S(1)}, bf16[4,4,4,2,4,8,128]{6,5,4,3,2,1,0:T(8,128)(2,1)S(1)}, bf16[4,4,4,2,3,8,128]{6,5,4,3,2,1...) custom-call(bf16[4,4,4,2,3,8,128]{6,5,4,3,2,1,0:T(8,128)(2,1)S(1)} %bitcast.37, ...), custom_call_target="tpu_custom_call" | custom-call | tf_op jit(solution)/shard_map/exchange/pallas_call | solution.py:338
  71.0 2.9 %finish.1 = (bf16[128,5,8,128]{3,2,1,0:T(8,128)(2,1)}, bf16[128,5120]{1,0:T(8,128)(2,1)}, f32[5,8,128]{2,1,0:T(8,128)}, f32[5,8,128]{2,1,0:T(8,128)}, f32[5,8,12...) custom-call(bf16[128,3,8,128]{3,2,1,0:T(8,128)(2,1)S(1)} %bitcast.35, ...), custom_call_target="tpu_custom_call" | custom-call | tf_op jit(solution)/shard_map/finish/pallas_call | solution.py:411
Async XLA Ops:
  0.6 1.0 %copy-start = (bf16[1024,128]{1,0:T(8,128)(2,1)S(1)}, bf16[1024,128]{1,0:T(8,128)(2,1)}, u32[]{:S(2)}) copy-start(bf16[1024,128]{1,0:T(8,128)(2,1)} %qc_hbm.1) | copy-start | bytes 786436
  1.6 0.9 %copy-start.1 = (bf16[1024,128]{1,0:T(8,128)(2,1)S(1)}, bf16[1024,128]{1,0:T(8,128)(2,1)}, u32[]{:S(2)}) copy-start(bf16[1024,128]{1,0:T(8,128)(2,1)} %ho_hbm.1) | copy-start | bytes 786436
  2.5 0.7 copy-start.2
  3.3 15.9 %copy-start.3 = (f32[40,128]{1,0:T(8,128)S(1)}, f32[40,128]{1,0:T(8,128)}, u32[]{:S(2)}) copy-start(f32[40,128]{1,0:T(8,128)} %param.16) | copy-start | bytes 61444
  3.3 15.9 %copy-start.4 = (f32[40,128]{1,0:T(8,128)S(1)}, f32[40,128]{1,0:T(8,128)}, u32[]{:S(2)}) copy-start(f32[40,128]{1,0:T(8,128)} %param.17) | copy-start | bytes 61444
  3.3 15.9 %copy-start.5 = (f32[40,128]{1,0:T(8,128)S(1)}, f32[40,128]{1,0:T(8,128)}, u32[]{:S(2)}) copy-start(f32[40,128]{1,0:T(8,128)} %param.18) | copy-start | bytes 61444
  3.3 15.9 %copy-start.6 = (f32[128,40]{0,1:T(8,128)S(1)}, f32[128,40]{0,1:T(8,128)}, u32[]{:S(2)}) copy-start(f32[128,40]{0,1:T(8,128)} %param.19) | copy-start | bytes 61444
  3.3 15.9 %copy-start.7 = (f32[128,40]{0,1:T(8,128)S(1)}, f32[128,40]{0,1:T(8,128)}, u32[]{:S(2)}) copy-start(f32[128,40]{0,1:T(8,128)} %param.20) | copy-start | bytes 61444
  3.3 15.9 %copy-start.8 = (f32[128,40]{0,1:T(8,128)S(1)}, f32[128,40]{0,1:T(8,128)}, u32[]{:S(2)}) copy-start(f32[128,40]{0,1:T(8,128)} %param.21) | copy-start | bytes 61444

commit v3 on v2

v3 whole, which is shorter than its diff:
```python
import functools
import math

import jax
import jax.numpy as jnp
from jax import lax
from jax.experimental import pallas as pl
from jax.experimental.pallas import tpu as pltpu
from jax.sharding import Mesh
from jax.sharding import PartitionSpec as P

D = 5120
WIDTH = 128
STEP = 20
TOK = 1024
DP = ("z", "y", "x", "c")

norm_eps = 1e-05
beta_one = 0.9
beta_two = 0.95
learn_rate = 0.001
decay_rate = 0.1
adam_eps = 1e-08
clip_rms = 1.0

F32 = jnp.float32
BF16 = jnp.bfloat16
MESH = pl.DeviceIdType.MESH

Q_CUT = ((0, 2), (2, 4), (4, 5))
O_CUT = ((0, 1), (1, 3), (3, 5))
TILES = tuple(q[1] - q[0] + o[1] - o[0] for q, o in zip(Q_CUT, O_CUT))
ORDER = (("x", "y", "z"), ("y", "z", "x"), ("z", "x", "y"))

SPAN = 1280
HALF = SPAN // 2
BLOCK = 128
ROWS = 16


def adamw(master, moment, second, gradient, factor):
    clipped = gradient * factor
    moment_new = beta_one * moment + (1.0 - beta_one) * clipped
    second_new = beta_two * second + (1.0 - beta_two) * clipped * clipped
    first_fix = 1.0 - beta_one**STEP
    second_fix = 1.0 - beta_two**STEP
    update = moment_new / first_fix / (jnp.sqrt(second_new / second_fix) + adam_eps)
    master_new = master - learn_rate * (update + decay_rate * master)
    return (master_new, moment_new, second_new)


def step_kernel(*refs):
    hidden, gain_hbm, qc_hbm, ho_hbm, oc = refs[0:5]
    olds = refs[5:11]
    pp = refs[11:14]
    news, rms_out = refs[14:16]
    scratch = refs[16:]
    hbuf, obuf, gain, qc, ho, qct, hot, states = scratch[0:8]
    full, got, half_sum = scratch[8:10], scratch[10:12], scratch[12:14]
    r1, s1, s1h, r2, s2, r3 = [scratch[14 + 3 * i : 17 + 3 * i] for i in range(6)]
    nall, hsem, osem, ssem, sem0, sem1, semr, semn, sema, semb, semc, semd = scratch[32:]

    me = {a: lax.axis_index(a) for a in DP}
    ring = {a: [me[a]] + [lax.rem(me[a] + j, 4) for j in (1, 2, 3)] for a in "zyx"}
    ring["c"] = [me["c"], 1 - me["c"]]
    back = {a: [me[a]] + [lax.rem(me[a] + 4 - j, 4) for j in (1, 2, 3)] for a in "zyx"}

    def peer(axis, j):
        return tuple(ring[a][j] if a == axis else me[a] for a in DP)

    def remote(src, dst, sems, axis, j):
        return pltpu.make_async_remote_copy(
            src_ref=src, dst_ref=dst, send_sem=sems.at[0], recv_sem=sems.at[1],
            device_id=peer(axis, j), device_id_type=MESH,
        )

    others = [
        (ring["z"][dz], ring["y"][dy], ring["x"][dx], ring["c"][dc])
        for dz in (2, 3, 1, 0) for dy in (2, 3, 1, 0) for dx in (2, 3, 1, 0) for dc in (1, 0)
        if dz + dy + dx + dc > 0
    ]
    barrier = pltpu.get_barrier_semaphore()
    for device in others:
        pl.semaphore_signal(barrier, inc=1, device_id=device, device_id_type=MESH)

    small = [
        pltpu.make_async_copy(a, b, ssem.at[i])
        for i, (a, b) in enumerate(((ho_hbm, ho), (qc_hbm, qc), (gain_hbm, gain)))
    ]
    small += [pltpu.make_async_copy(olds[i], states.at[i], ssem.at[3 + i]) for i in range(6)]
    turns = (1, 2, 3, 0)

    def columns(j, half):
        return pl.ds(pl.multiple_of(ring["z"][j] * SPAN + half * HALF, 128), HALF)

    local = []
    for copy in small[:3]:
        copy.start()
    for i in range(8):
        cols = columns(turns[i // 2], i % 2)
        rows = slice(i * BLOCK, (i + 1) * BLOCK)
        local.append(
            (
                pltpu.make_async_copy(oc.at[:, cols], obuf.at[i], osem.at[i]),
                pltpu.make_async_copy(hidden.at[rows], hbuf.at[rows], hsem.at[i]),
            )
        )
        for copy in local[-1]:
            copy.start()
    for copy in small[3:]:
        copy.start()
    for copy in small[:3]:
        copy.wait()
    hot[...] = ho[...].astype(F32).T.astype(BF16)
    qct[...] = qc[...].astype(F32).T.astype(BF16)

    sends = []
    swaps = {}
    arrive = [[], [], []]

    def swap(which, j):
        zb = ring["z"][j]
        copy = remote(full[which].at[zb, :, :, ring["c"][1]], got[which].at[zb], sem0.at[which, j], "c", 1)
        copy.start()
        swaps[which, j] = copy
        sends.append(copy)

    def spread(which, j):
        zb = ring["z"][j]
        swaps[which, j].wait_recv()
        for y in range(4):
            chip = full[which][zb, y, :, me["c"]] + got[which][zb, y]
            half_sum[which][zb, y] = chip.astype(BF16)
        for k in range(3):
            lo, hi = (Q_CUT, O_CUT)[which][k]
            at = TILES[k] - (hi - lo) if which else 0
            axis = ORDER[k][0]
            tiles, spot = slice(lo, hi), slice(at, at + hi - lo)
            if axis == "z":
                if j:
                    copy = remote(
                        half_sum[which].at[zb, :, :, tiles], r1[k].at[j - 1, :, :, spot], sem1.at[k, which, j, 0], "z", j
                    )
                    copy.start()
                    sends.append(copy)
                    arrive[k].append(copy)
            else:
                for p in (1, 3, 2):
                    to = ring[axis][p]
                    src = half_sum[which].at[zb, :, to, tiles] if axis == "x" else half_sum[which].at[zb, to, :, tiles]
                    copy = remote(src, r1[k].at[p - 1, zb, :, spot], sem1.at[k, which, j, p - 1], axis, p)
                    copy.start()
                    sends.append(copy)
                    arrive[k].append(copy)

    previous = None
    for i in range(8):
        j, half = turns[i // 2], i % 2
        local[i][0].wait()
        local[i][1].wait()
        grad = jnp.dot(hot[...], obuf[i], preferred_element_type=F32)
        full[1][ring["z"][j], 2 * half : 2 * half + 2] = grad.T.reshape(2, 4, 2, 5, 8, WIDTH)
        for r in range(BLOCK // ROWS):
            rows = slice(i * BLOCK + r * ROWS, i * BLOCK + (r + 1) * ROWS)
            wide = hbuf[rows, :].astype(F32)
            mean = jnp.sum(wide * wide, axis=1, keepdims=True) * (1.0 / D)
            hbuf[rows, :] = (wide * lax.rsqrt(mean + norm_eps) * gain[...]).astype(BF16)
        if half:
            if i == 1:
                pl.semaphore_wait(barrier, len(others))
            swap(1, j)
            if previous is not None:
                spread(1, previous)
            previous = j
    for j in turns:
        cols = pl.ds(pl.multiple_of(ring["z"][j] * SPAN, 128), SPAN)
        grad = jnp.dot(qct[...], hbuf[:, cols], preferred_element_type=F32)
        full[0][ring["z"][j]] = grad.T.reshape(4, 4, 2, 5, 8, WIDTH)
        swap(0, j)
        if j == turns[0]:
            spread(1, turns[-1])
        else:
            spread(0, previous)
        previous = j
    spread(0, previous)

    third = [[], [], []]
    for k in range(3):
        for copy in arrive[k]:
            copy.wait_recv()
        axis = ORDER[k][0]
        left = "zyx".replace(axis, "")

        def add1(i, _, k=k, axis=axis):
            own = {"z": (me["z"], i), "y": (i, me["y"]), "x": (i, slice(None), me["x"])}[axis]
            mine = {"z": (me["z"], i, slice(None)), "y": (i, me["y"], slice(None)), "x": (i, slice(None), me["x"])}[axis]
            for which in range(2):
                lo, hi = (Q_CUT, O_CUT)[which][k]
                at = TILES[k] - (hi - lo) if which else 0
                total = full[which][mine + (me["c"], slice(lo, hi))] + got[which][own + (slice(None),) * (3 - len(own)) + (slice(lo, hi),)]
                for j in range(3):
                    total = total + r1[k][j, i, :, at : at + hi - lo].astype(F32)
                s1[k][i, :, at : at + hi - lo] = total
                s1h[k][i, :, at : at + hi - lo] = total.astype(BF16)
            return 0

        lax.fori_loop(0, 4, add1, 0)
        axis = ORDER[k][1]
        for j in (1, 3, 2):
            src = s1h[k].at[ring[axis][j]] if left.index(axis) == 0 else s1h[k].at[:, ring[axis][j]]
            copy = remote(src, r2[k].at[j - 1], semr.at[k, 0, j - 1], axis, j)
            copy.start()
            third[k].append(copy)
            sends.append(copy)
    fourth = [[], [], []]
    for k in range(3):
        for copy in third[k]:
            copy.wait_recv()
        left = "zyx".replace(ORDER[k][0], "")
        axis = ORDER[k][1]
        own = me[axis] if left.index(axis) == 0 else (slice(None), me[axis])
        total = s1[k][own]
        for j in range(3):
            total = total + r2[k][j].astype(F32)
        s2[k][...] = total
        axis = ORDER[k][2]
        for j in (1, 3, 2):
            copy = remote(s2[k].at[ring[axis][j]], r3[k].at[j - 1], semr.at[k, 1, j - 1], axis, j)
            copy.start()
            fourth[k].append(copy)
            sends.append(copy)
    grads = []
    square = jnp.zeros((8, 128), F32)
    for k in range(3):
        for copy in fourth[k]:
            copy.wait_recv()
        total = s2[k][me[ORDER[k][2]]]
        for j in range(3):
            total = total + r3[k][j]
        grads.append(total)
        square = square + jnp.sum(total * total, axis=0)

    number = ((me["z"] * 4 + me["y"]) * 4 + me["x"]) * 2 + me["c"]
    mine = nall.at[pl.ds(number, 1)]
    nall[pl.ds(number, 1), :] = jnp.sum(square, axis=0, keepdims=True)
    for device in others:
        pltpu.make_async_remote_copy(
            src_ref=mine, dst_ref=mine, send_sem=semn.at[0], recv_sem=semn.at[1],
            device_id=device, device_id_type=MESH,
        ).start()
    rest = nall.at[pl.ds(0, len(others))]
    every = remote(rest, rest, semn, "c", 1)
    every.wait_recv()
    square = nall[...]
    total_square = jnp.sum(jnp.sum(square, axis=0, keepdims=True), axis=1, keepdims=True)
    rms = jnp.sqrt(total_square / (2.0 * D * WIDTH))
    rms_out[...] = rms
    factor = jnp.minimum(1.0, clip_rms / rms)

    here = (me["z"], me["y"], me["x"], me["c"])
    for copy in small[3:]:
        copy.wait()
    for k in range(3):
        for which, cuts in enumerate((Q_CUT, O_CUT)):
            lo, hi = cuts[k]
            at = TILES[k] - (hi - lo) if which else 0
            prior = [states[3 * which + i, lo:hi] for i in range(3)]
            fresh = adamw(*prior, grads[k][at : at + hi - lo], factor)
            for i in range(3):
                news[3 * which + i, lo:hi] = fresh[i]
            pp[k][here + (slice(at, at + hi - lo),)] = fresh[0].astype(BF16)

    def block(k, i, j, every=True):
        one, two, three = ORDER[k]
        index = dict(me)
        index[one], index[two] = back[one][i], back[two][j]
        if every:
            index[three] = slice(None)
        return pp[k].at[tuple(index[a] for a in DP)]

    along3, along2, along1, cross = [{} for _ in range(4)]

    def go(kept, key, ref, sems, axis, j):
        kept[key] = remote(ref, ref, sems, axis, j)
        kept[key].start()
        sends.append(kept[key])

    near = (1, 3, 2)
    for k in range(3):
        for j in near:
            go(along3, (k, j), block(k, 0, 0, False), sema.at[k, j - 1], ORDER[k][2], j)
    for k in range(3):
        for j in near:
            along3[k, j].wait_recv()
        for j in near:
            go(along2, (k, j), block(k, 0, 0), semb.at[k, j - 1], ORDER[k][1], j)
        for j in near:
            go(along1, (k, 0, j), block(k, 0, 0), semc.at[k, 0, j - 1], ORDER[k][0], j)
        go(cross, (k, 0, 0), block(k, 0, 0), semd.at[k, 0, 0], "c", 1)
    for two in near:
        for k in range(3):
            along2[k, two].wait_recv()
            for j in near:
                go(along1, (k, two, j), block(k, 0, two), semc.at[k, two, j - 1], ORDER[k][0], j)
            go(cross, (k, 0, two), block(k, 0, two), semd.at[k, 0, two], "c", 1)
    for two in (0,) + near:
        for j in near:
            for k in range(3):
                along1[k, two, j].wait_recv()
                go(cross, (k, j, two), block(k, j, two), semd.at[k, j, two], "c", 1)
    for copy in cross.values():
        copy.wait_recv()
    every.wait_send()
    for copy in sends:
        copy.wait_send()


def step(operands, states):
    vmem = pl.BlockSpec(memory_space=pltpu.VMEM)
    hbm = pl.BlockSpec(memory_space=pltpu.HBM)
    per = lambda lead, dtype: [pltpu.VMEM(lead + (t, 8, 128), dtype) for t in TILES]
    dma = pltpu.SemaphoreType.DMA
    return pl.pallas_call(
        step_kernel,
        out_shape=[pltpu.VMEM((4, 4, 4, 2, t, 8, 128), BF16) for t in TILES]
        + [pltpu.VMEM((6, 5, 8, 128), F32), jax.ShapeDtypeStruct((1, 1), F32)],
        in_specs=[hbm] * 11,
        out_specs=[vmem] * 5,
        scratch_shapes=[
            pltpu.VMEM((TOK, D), BF16),
            pltpu.VMEM((8, TOK, HALF), BF16),
            pltpu.VMEM((1, D), F32),
            pltpu.VMEM((TOK, 128), BF16),
            pltpu.VMEM((TOK, 128), BF16),
            pltpu.VMEM((128, TOK), BF16),
            pltpu.VMEM((128, TOK), BF16),
            pltpu.VMEM((6, 5, 8, 128), F32),
        ]
        + [pltpu.VMEM((4, 4, 4, 2, 5, 8, 128), F32)] * 2
        + [pltpu.VMEM((4, 4, 4, 5, 8, 128), F32)] * 2
        + [pltpu.VMEM((4, 4, 4, 5, 8, 128), BF16)] * 2
        + per((3, 4, 4), BF16)
        + per((4, 4), F32)
        + per((4, 4), BF16)
        + per((3, 4), BF16)
        + per((4,), F32)
        + per((3,), F32)
        + [
            pltpu.VMEM((128, 128), F32),
            dma((8,)),
            dma((8,)),
            dma((9,)),
            dma((2, 4, 2)),
            dma((3, 2, 4, 3, 2)),
            dma((3, 2, 3, 2)),
            dma((2,)),
            dma((3, 3, 2)),
            dma((3, 3, 2)),
            dma((3, 4, 3, 2)),
            dma((3, 4, 4, 2)),
        ],
        compiler_params=pltpu.CompilerParams(
            collective_id=0, has_side_effects=True, vmem_limit_bytes=58 * 1024 * 1024
        ),
        cost_estimate=pl.CostEstimate(flops=4 * TOK * D * 128, bytes_accessed=4 * TOK * D, transcendentals=0),
        name="step",
    )(*operands, *states)


GROUP = 16


def finish_kernel(p_a, p_b, p_c, news, rms, q_out, o_out, *rest):
    outs, rms_out = rest[:6], rest[6]
    turned, qsem, nsem, osem = rest[7:]
    pp = (p_a, p_b, p_c)
    copies = []

    def go(src, dst, sem):
        copies.append(pltpu.make_async_copy(src, dst, sem))
        copies[-1].start()

    for k in range(3):
        lo, hi = Q_CUT[k]
        go(pp[k].at[:, 0 : hi - lo], q_out.at[:, lo:hi], qsem.at[k])
    for i in range(6):
        go(news.at[i], outs[i], nsem.at[i])
    rms_out[...] = rms[...]
    where = {}
    for k in range(3):
        lo, hi = O_CUT[k]
        for t in range(lo, hi):
            where[t] = (k, TILES[k] - hi + t)
    for group in range(128 // GROUP):
        for b in range(5):
            tiles = []
            for i in range(16):
                flat = b * 16 + i
                k, t = where[flat % 5]
                tiles.append(pp[k][group * GROUP + flat // 5, t].astype(F32))
            wide = jnp.concatenate(tiles, axis=0).T
            at = group * 640 + b * 128
            turned[:, at : at + 128] = wide.astype(BF16)
        cols = slice(group * 640, (group + 1) * 640)
        go(turned.at[:, cols], o_out.at[:, cols], osem.at[group])
    for copy in copies:
        copy.wait()


def finish(pp, news, rms):
    vmem = pl.BlockSpec(memory_space=pltpu.VMEM)
    hbm = pl.BlockSpec(memory_space=pltpu.HBM)
    return pl.pallas_call(
        finish_kernel,
        out_shape=[jax.ShapeDtypeStruct((128, 5, 8, 128), BF16), jax.ShapeDtypeStruct((WIDTH, D), BF16)]
        + [jax.ShapeDtypeStruct((5, 8, 128), F32)] * 6
        + [jax.ShapeDtypeStruct((1, 1), F32)],
        in_specs=[vmem] * 5,
        out_specs=[hbm] * 8 + [vmem],
        scratch_shapes=[
            pltpu.VMEM((WIDTH, D), BF16),
            pltpu.SemaphoreType.DMA((3,)),
            pltpu.SemaphoreType.DMA((6,)),
            pltpu.SemaphoreType.DMA((128 // GROUP,)),
        ],
        compiler_params=pltpu.CompilerParams(vmem_limit_bytes=16 * 1024 * 1024),
        name="finish",
    )(*pp, news, rms)


def shards(hidden, norm_gain, q_cotangent, head_output, out_cotangent, master_q, moment_q, second_q, master_o, moment_o, second_o):
    states = [a.reshape(5, 8, 128) for a in (master_q, moment_q, second_q, master_o.T, moment_o.T, second_o.T)]
    out = step((hidden, norm_gain.reshape(1, D), q_cotangent, head_output, out_cotangent), states)
    out = finish([a.reshape(128, *a.shape[4:]) for a in out[:3]], out[3], out[4])
    fresh = [a.reshape(40, 128) for a in out[2:8]]
    return (out[0].reshape(D, WIDTH), out[1], *fresh[:3], *[a.T for a in fresh[3:]], out[8].reshape(()))


def solution(mesh):
    split = Mesh(mesh.devices.reshape(4, 4, 4, 2), DP)
    tall, wide, whole = P(DP, None), P(None, DP), P()
    return jax.shard_map(
        shards,
        mesh=split,
        in_specs=(tall, whole, tall, tall, tall, tall, tall, tall, wide, wide, wide),
        out_specs=(whole, whole, tall, tall, tall, wide, wide, wide, whole),
        check_vma=False,
    )
```

time: 74.1 us -> 60.6 us (0.82)
  Pallas kernels: 70.5 us -> 59.7 us
  local copies, waits for them, and re-layouts: 2.64 us -> 0 us
    pallas_call x2 -> x1, Pallas kernels: 67.6 us -> 56.8 us  [step(): pl.pallas_call(step_kernel, out_shape=[pltpu.VMEM((4, 4, 4, 2, t, 8, 128)...]
    unnamed x18 -> x0, local copies, waits for them, and re-layouts: 2.64 us -> none
where the time goes in v3:
time: 60.6 us; the launch traced here: 60.5 us
  Pallas kernels  59.7 us (99%)
  between operations  0.81 us (1%)
    pallas_call x1, Pallas kernels, step(): pl.pallas_call(step_kernel, out_shape=[pltpu.VMEM((4, 4, 4, 2, t, 8, 128)...  56.8 us
    pallas_call x1, Pallas kernels, finish(): pl.pallas_call(finish_kernel, out_shape=[jax.ShapeDtypeStruct((128, 5, 8,...  2.94 us

profile of v3, /device:TPU:1, one launch (start us, length us, event | category | flops | bytes accessed | tf_op | source)
XLA Modules:
  0.0 60.5 jit_solution(1239466903802633461)
XLA Ops:
  0.6 56.8 %step.1 = (bf16[4,4,4,2,3,8,128]{6,5,4,3,2,1,0:T(8,128)(2,1)S(1)}, bf16[4,4,4,2,4,8,128]{6,5,4,3,2,1,0:T(8,128)(2,1)S(1)}, bf16[4,4,4,2,3,8,128]{6,5,4,3,2,1,0:T...) custom-call(bf16[1024,5120]{1,0:T(8,128)(2,1)} %refs_0_.1, f32[1,5120]{1,0:T(1,128)} %bitcast.33, ...), custom_call_target="tpu_custom_call" | custom-call | flops 2684354560 | bytes 20971520 | tf_op jit(solution)/shard_map/step/pallas_call | solution.py:323
  57.4 2.9 %finish.1 = (bf16[128,5,8,128]{3,2,1,0:T(8,128)(2,1)}, bf16[128,5120]{1,0:T(8,128)(2,1)}, f32[5,8,128]{2,1,0:T(8,128)}, f32[5,8,128]{2,1,0:T(8,128)}, f32[5,8,12...) custom-call(bf16[128,3,8,128]{3,2,1,0:T(8,128)(2,1)S(1)} %bitcast.31, ...), custom_call_target="tpu_custom_call" | custom-call | tf_op jit(solution)/shard_map/finish/pallas_call | solution.py:413

commit v4 on v3

--- a/solution.py
+++ b/solution.py
@@ -58,7 +58,7 @@
     hbuf, obuf, gain, qc, ho, qct, hot, states = scratch[0:8]
     full, got, half_sum = scratch[8:10], scratch[10:12], scratch[12:14]
     r1, s1, s1h, r2, s2, r3 = [scratch[14 + 3 * i : 17 + 3 * i] for i in range(6)]
-    nall, hsem, osem, ssem, sem0, sem1, semr, semn, sema, semb, semc, semd = scratch[32:]
+    nall, hsem, osem, ssem, swap_sent, swap_got, pairs, two_got, one_got, near_sent, semn = scratch[32:]
 
     me = {a: lax.axis_index(a) for a in DP}
     ring = {a: [me[a]] + [lax.rem(me[a] + j, 4) for j in (1, 2, 3)] for a in "zyx"}
@@ -68,11 +68,22 @@
     def peer(axis, j):
         return tuple(ring[a][j] if a == axis else me[a] for a in DP)
 
-    def remote(src, dst, sems, axis, j):
+    def remote(src, dst, sent, got_sem, axis, j):
         return pltpu.make_async_remote_copy(
-            src_ref=src, dst_ref=dst, send_sem=sems.at[0], recv_sem=sems.at[1],
+            src_ref=src, dst_ref=dst, send_sem=sent, recv_sem=got_sem,
             device_id=peer(axis, j), device_id_type=MESH,
         )
+
+    drains = []
+
+    def whole(ref, sent, got_sem, drain=True):
+        every = remote(ref, ref, sent, got_sem, "c", 1)
+        if drain:
+            drains.append(every)
+        return every
+
+    def pair(stage, k):
+        return pairs.at[stage, k, 0], pairs.at[stage, k, 1]
 
     others = [
         (ring["z"][dz], ring["y"][dy], ring["x"][dx], ring["c"][dc])
@@ -87,7 +98,7 @@
         pltpu.make_async_copy(a, b, ssem.at[i])
         for i, (a, b) in enumerate(((ho_hbm, ho), (qc_hbm, qc), (gain_hbm, gain)))
     ]
-    small += [pltpu.make_async_copy(olds[i], states.at[i], ssem.at[3 + i]) for i in range(6)]
+    small += [pltpu.make_async_copy(olds[i], states.at[i], ssem.at[3]) for i in range(6)]
     turns = (1, 2, 3, 0)
 
     def columns(j, half):
@@ -114,20 +125,15 @@
     hot[...] = ho[...].astype(F32).T.astype(BF16)
     qct[...] = qc[...].astype(F32).T.astype(BF16)
 
-    sends = []
-    swaps = {}
-    arrive = [[], [], []]
 
     def swap(which, j):
         zb = ring["z"][j]
-        copy = remote(full[which].at[zb, :, :, ring["c"][1]], got[which].at[zb], sem0.at[which, j], "c", 1)
-        copy.start()
-        swaps[which, j] = copy
-        sends.append(copy)
+        src = full[which].at[zb, :, :, ring["c"][1]]
+        remote(src, got[which].at[zb], swap_sent.at[which], swap_got.at[which, j], "c", 1).start()
 
     def spread(which, j):
         zb = ring["z"][j]
-        swaps[which, j].wait_recv()
+        whole(got[which].at[zb], swap_sent.at[which], swap_got.at[which, j], False).wait_recv()
         for y in range(4):
             chip = full[which][zb, y, :, me["c"]] + got[which][zb, y]
             half_sum[which][zb, y] = chip.astype(BF16)
@@ -138,20 +144,14 @@
             tiles, spot = slice(lo, hi), slice(at, at + hi - lo)
             if axis == "z":
                 if j:
-                    copy = remote(
-                        half_sum[which].at[zb, :, :, tiles], r1[k].at[j - 1, :, :, spot], sem1.at[k, which, j, 0], "z", j
-                    )
-                    copy.start()
-                    sends.append(copy)
-                    arrive[k].append(copy)
+                    remote(
+                        half_sum[which].at[zb, :, :, tiles], r1[k].at[j - 1, :, :, spot], *pair(0, k), "z", j
+                    ).start()
             else:
                 for p in (1, 3, 2):
                     to = ring[axis][p]
                     src = half_sum[which].at[zb, :, to, tiles] if axis == "x" else half_sum[which].at[zb, to, :, tiles]
-                    copy = remote(src, r1[k].at[p - 1, zb, :, spot], sem1.at[k, which, j, p - 1], axis, p)
-                    copy.start()
-                    sends.append(copy)
-                    arrive[k].append(copy)
+                    remote(src, r1[k].at[p - 1, zb, :, spot], *pair(0, k), axis, p).start()
 
     previous = None
     for i in range(8):
@@ -184,10 +184,10 @@
         previous = j
     spread(0, previous)
 
-    third = [[], [], []]
-    for k in range(3):
-        for copy in arrive[k]:
-            copy.wait_recv()
+    for which in range(2):
+        whole(got[which], swap_sent.at[which], swap_got.at[which, 0])
+    for k in range(3):
+        whole(r1[k], *pair(0, k)).wait_recv()
         axis = ORDER[k][0]
         left = "zyx".replace(axis, "")
 
@@ -208,14 +208,9 @@
         axis = ORDER[k][1]
         for j in (1, 3, 2):
             src = s1h[k].at[ring[axis][j]] if left.index(axis) == 0 else s1h[k].at[:, ring[axis][j]]
-            copy = remote(src, r2[k].at[j - 1], semr.at[k, 0, j - 1], axis, j)
-            copy.start()
-            third[k].append(copy)
-            sends.append(copy)
-    fourth = [[], [], []]
-    for k in range(3):
-        for copy in third[k]:
-            copy.wait_recv()
+            remote(src, r2[k].at[j - 1], *pair(1, k), axis, j).start()
+    for k in range(3):
+        whole(r2[k], *pair(1, k)).wait_recv()
         left = "zyx".replace(ORDER[k][0], "")
         axis = ORDER[k][1]
         own = me[axis] if left.index(axis) == 0 else (slice(None), me[axis])
@@ -225,15 +220,11 @@
         s2[k][...] = total
         axis = ORDER[k][2]
         for j in (1, 3, 2):
-            copy = remote(s2[k].at[ring[axis][j]], r3[k].at[j - 1], semr.at[k, 1, j - 1], axis, j)
-            copy.start()
-            fourth[k].append(copy)
-            sends.append(copy)
+            remote(s2[k].at[ring[axis][j]], r3[k].at[j - 1], *pair(2, k), axis, j).start()
     grads = []
     square = jnp.zeros((8, 128), F32)
     for k in range(3):
-        for copy in fourth[k]:
-            copy.wait_recv()
+        whole(r3[k], *pair(2, k)).wait_recv()
         total = s2[k][me[ORDER[k][2]]]
         for j in range(3):
             total = total + r3[k][j]
@@ -249,8 +240,7 @@
             device_id=device, device_id_type=MESH,
         ).start()
     rest = nall.at[pl.ds(0, len(others))]
-    every = remote(rest, rest, semn, "c", 1)
-    every.wait_recv()
+    whole(rest, semn.at[0], semn.at[1]).wait_recv()
     square = nall[...]
     total_square = jnp.sum(jnp.sum(square, axis=0, keepdims=True), axis=1, keepdims=True)
     rms = jnp.sqrt(total_square / (2.0 * D * WIDTH))
@@ -258,8 +248,7 @@
     factor = jnp.minimum(1.0, clip_rms / rms)
 
     here = (me["z"], me["y"], me["x"], me["c"])
-    for copy in small[3:]:
-        copy.wait()
+    pltpu.make_async_copy(states, states, ssem.at[3]).wait()
     for k in range(3):
         for which, cuts in enumerate((Q_CUT, O_CUT)):
             lo, hi = cuts[k]
@@ -278,41 +267,39 @@
             index[three] = slice(None)
         return pp[k].at[tuple(index[a] for a in DP)]
 
-    along3, along2, along1, cross = [{} for _ in range(4)]
-
-    def go(kept, key, ref, sems, axis, j):
-        kept[key] = remote(ref, ref, sems, axis, j)
-        kept[key].start()
-        sends.append(kept[key])
+    def go(ref, sent, got_sem, axis, j):
+        remote(ref, ref, sent, got_sem, axis, j).start()
 
     near = (1, 3, 2)
     for k in range(3):
         for j in near:
-            go(along3, (k, j), block(k, 0, 0, False), sema.at[k, j - 1], ORDER[k][2], j)
-    for k in range(3):
+            go(block(k, 0, 0, False), *pair(3, k), ORDER[k][2], j)
+    for k in range(3):
+        whole(pp[k].at[0, 0, 0:3, 0], *pair(3, k)).wait_recv()
+        mine = block(k, 0, 0)
         for j in near:
-            along3[k, j].wait_recv()
+            go(mine, near_sent.at[0, k], two_got.at[k, j - 1], ORDER[k][1], j)
         for j in near:
-            go(along2, (k, j), block(k, 0, 0), semb.at[k, j - 1], ORDER[k][1], j)
-        for j in near:
-            go(along1, (k, 0, j), block(k, 0, 0), semc.at[k, 0, j - 1], ORDER[k][0], j)
-        go(cross, (k, 0, 0), block(k, 0, 0), semd.at[k, 0, 0], "c", 1)
+            go(mine, near_sent.at[1, k], one_got.at[k, 0], ORDER[k][0], j)
+        go(mine, *pair(4, k), "c", 1)
     for two in near:
         for k in range(3):
-            along2[k, two].wait_recv()
+            theirs = block(k, 0, two)
+            whole(theirs, near_sent.at[0, k], two_got.at[k, two - 1], False).wait_recv()
             for j in near:
-                go(along1, (k, two, j), block(k, 0, two), semc.at[k, two, j - 1], ORDER[k][0], j)
-            go(cross, (k, 0, two), block(k, 0, two), semd.at[k, 0, two], "c", 1)
+                go(theirs, near_sent.at[1, k], one_got.at[k, two], ORDER[k][0], j)
+            go(theirs, *pair(4, k), "c", 1)
     for two in (0,) + near:
-        for j in near:
-            for k in range(3):
-                along1[k, two, j].wait_recv()
-                go(cross, (k, j, two), block(k, j, two), semd.at[k, j, two], "c", 1)
-    for copy in cross.values():
-        copy.wait_recv()
-    every.wait_send()
-    for copy in sends:
-        copy.wait_send()
+        for k in range(3):
+            whole(pp[k].at[0, 0:3, :, 0], near_sent.at[1, k], one_got.at[k, two], False).wait_recv()
+            for j in near:
+                go(block(k, j, two), *pair(4, k), "c", 1)
+    for k in range(3):
+        whole(pp[k].at[:, :, :, 0], *pair(4, k)).wait_recv()
+        whole(pp[k].at[0, 0:3, :, 0], near_sent.at[0, k], two_got.at[k, 0])
+        whole(pp[k].at[0:3, :, :, 0], near_sent.at[1, k], one_got.at[k, 0])
+    for every in drains:
+        every.wait_send()
 
 
 def step(operands, states):
@@ -349,15 +336,14 @@
             pltpu.VMEM((128, 128), F32),
             dma((8,)),
             dma((8,)),
-            dma((9,)),
-            dma((2, 4, 2)),
-            dma((3, 2, 4, 3, 2)),
-            dma((3, 2, 3, 2)),
+            dma((4,)),
             dma((2,)),
-            dma((3, 3, 2)),
-            dma((3, 3, 2)),
-            dma((3, 4, 3, 2)),
-            dma((3, 4, 4, 2)),
+            dma((2, 4)),
+            dma((5, 3, 2)),
+            dma((3, 3)),
+            dma((3, 4)),
+            dma((2, 3)),
+            dma((2,)),
         ],
         compiler_params=pltpu.CompilerParams(
             collective_id=0, has_side_effects=True, vmem_limit_bytes=58 * 1024 * 1024

time: 60.6 us -> 57.3 us (0.946)
  Pallas kernels: 59.7 us -> 56.5 us
    pallas_call x1, Pallas kernels: 56.8 us -> 53.6 us  [step(): pl.pallas_call(step_kernel, out_shape=[pltpu.VMEM((4, 4, 4, 2, t, 8, 128)...]
where the time goes in v4:
time: 57.3 us; the launch traced here: 57.2 us
  Pallas kernels  56.5 us (99%)
  between operations  0.65 us (1%)
    pallas_call x1, Pallas kernels, step(): pl.pallas_call(step_kernel, out_shape=[pltpu.VMEM((4, 4, 4, 2, t, 8, 128)...  53.6 us
    pallas_call x1, Pallas kernels, finish(): pl.pallas_call(finish_kernel, out_shape=[jax.ShapeDtypeStruct((128, 5, 8,...  2.94 us

profile of v4, /device:TPU:1, one launch (start us, length us, event | category | flops | bytes accessed | tf_op | source)
XLA Modules:
  0.0 57.2 jit_solution(5940841781691560077)
XLA Ops:
  0.6 53.6 %step.1 = (bf16[4,4,4,2,3,8,128]{6,5,4,3,2,1,0:T(8,128)(2,1)S(1)}, bf16[4,4,4,2,4,8,128]{6,5,4,3,2,1,0:T(8,128)(2,1)S(1)}, bf16[4,4,4,2,3,8,128]{6,5,4,3,2,1,0:T...) custom-call(bf16[1024,5120]{1,0:T(8,128)(2,1)} %refs_0_.1, f32[1,5120]{1,0:T(1,128)} %bitcast.33, ...), custom_call_target="tpu_custom_call" | custom-call | flops 2684354560 | bytes 20971520 | tf_op jit(solution)/shard_map/step/pallas_call | solution.py:310
  54.2 2.9 %finish.1 = (bf16[128,5,8,128]{3,2,1,0:T(8,128)(2,1)}, bf16[128,5120]{1,0:T(8,128)(2,1)}, f32[5,8,128]{2,1,0:T(8,128)}, f32[5,8,128]{2,1,0:T(8,128)}, f32[5,8,12...) custom-call(bf16[128,3,8,128]{3,2,1,0:T(8,128)(2,1)S(1)} %bitcast.31, ...), custom_call_target="tpu_custom_call" | custom-call | tf_op jit(solution)/shard_map/finish/pallas_call | solution.py:399

commit v5 on v4

--- a/solution.py
+++ b/solution.py
@@ -57,8 +57,8 @@
     scratch = refs[16:]
     hbuf, obuf, gain, qc, ho, qct, hot, states = scratch[0:8]
     full, got, half_sum = scratch[8:10], scratch[10:12], scratch[12:14]
-    r1, s1, s1h, r2, s2, r3 = [scratch[14 + 3 * i : 17 + 3 * i] for i in range(6)]
-    nall, hsem, osem, ssem, swap_sent, swap_got, pairs, two_got, one_got, near_sent, semn = scratch[32:]
+    r1, s1, s1h, r2 = [scratch[14 + 3 * i : 17 + 3 * i] for i in range(4)]
+    nall, hsem, osem, ssem, swap_sent, swap_got, pairs, two_got, one_got, near_sent, semn = scratch[26:]
 
     me = {a: lax.axis_index(a) for a in DP}
     ring = {a: [me[a]] + [lax.rem(me[a] + j, 4) for j in (1, 2, 3)] for a in "zyx"}
@@ -148,7 +148,7 @@
                         half_sum[which].at[zb, :, :, tiles], r1[k].at[j - 1, :, :, spot], *pair(0, k), "z", j
                     ).start()
             else:
-                for p in (1, 3, 2):
+                for p in (2, 1, 3):
                     to = ring[axis][p]
                     src = half_sum[which].at[zb, :, to, tiles] if axis == "x" else half_sum[which].at[zb, to, :, tiles]
                     remote(src, r1[k].at[p - 1, zb, :, spot], *pair(0, k), axis, p).start()
@@ -205,29 +205,26 @@
             return 0
 
         lax.fori_loop(0, 4, add1, 0)
-        axis = ORDER[k][1]
-        for j in (1, 3, 2):
-            src = s1h[k].at[ring[axis][j]] if left.index(axis) == 0 else s1h[k].at[:, ring[axis][j]]
-            remote(src, r2[k].at[j - 1], *pair(1, k), axis, j).start()
+        two, three = ORDER[k][1:]
+        for j in (2, 1, 3, 0):
+            for i in (2, 1, 3, 0):
+                if i + j == 0:
+                    continue
+                at = dict(me)
+                at[two], at[three] = ring[two][j], ring[three][i]
+                pltpu.make_async_remote_copy(
+                    src_ref=s1h[k].at[tuple(at[a] for a in left)], dst_ref=r2[k].at[4 * j + i - 1],
+                    send_sem=pairs.at[1, k, 0], recv_sem=pairs.at[1, k, 1],
+                    device_id=tuple(at[a] for a in DP), device_id_type=MESH,
+                ).start()
+    grads = []
+    square = jnp.zeros((8, 128), F32)
     for k in range(3):
         whole(r2[k], *pair(1, k)).wait_recv()
         left = "zyx".replace(ORDER[k][0], "")
-        axis = ORDER[k][1]
-        own = me[axis] if left.index(axis) == 0 else (slice(None), me[axis])
-        total = s1[k][own]
-        for j in range(3):
-            total = total + r2[k][j].astype(F32)
-        s2[k][...] = total
-        axis = ORDER[k][2]
-        for j in (1, 3, 2):
-            remote(s2[k].at[ring[axis][j]], r3[k].at[j - 1], *pair(2, k), axis, j).start()
-    grads = []
-    square = jnp.zeros((8, 128), F32)
-    for k in range(3):
-        whole(r3[k], *pair(2, k)).wait_recv()
-        total = s2[k][me[ORDER[k][2]]]
-        for j in range(3):
-            total = total + r3[k][j]
+        total = s1[k][tuple(me[a] for a in left)]
+        for n in range(15):
+            total = total + r2[k][n].astype(F32)
         grads.append(total)
         square = square + jnp.sum(total * total, axis=0)
 
@@ -271,22 +268,30 @@
         remote(ref, ref, sent, got_sem, axis, j).start()
 
     near = (1, 3, 2)
-    for k in range(3):
-        for j in near:
-            go(block(k, 0, 0, False), *pair(3, k), ORDER[k][2], j)
+    far = (2, 1, 3)
+    for k in range(3):
+        share = block(k, 0, 0, False)
+        for j in far:
+            go(share, *pair(3, k), ORDER[k][2], j)
+        for j in far:
+            for i in (2, 1, 3, 0):
+                at = dict(me)
+                at[ORDER[k][1]], at[ORDER[k][2]] = ring[ORDER[k][1]][j], ring[ORDER[k][2]][i]
+                pltpu.make_async_remote_copy(
+                    src_ref=share, dst_ref=share, send_sem=near_sent.at[0, k], recv_sem=two_got.at[k, j - 1],
+                    device_id=tuple(at[a] for a in DP), device_id_type=MESH,
+                ).start()
     for k in range(3):
         whole(pp[k].at[0, 0, 0:3, 0], *pair(3, k)).wait_recv()
         mine = block(k, 0, 0)
-        for j in near:
-            go(mine, near_sent.at[0, k], two_got.at[k, j - 1], ORDER[k][1], j)
-        for j in near:
+        for j in far:
             go(mine, near_sent.at[1, k], one_got.at[k, 0], ORDER[k][0], j)
         go(mine, *pair(4, k), "c", 1)
     for two in near:
         for k in range(3):
             theirs = block(k, 0, two)
             whole(theirs, near_sent.at[0, k], two_got.at[k, two - 1], False).wait_recv()
-            for j in near:
+            for j in far:
                 go(theirs, near_sent.at[1, k], one_got.at[k, two], ORDER[k][0], j)
             go(theirs, *pair(4, k), "c", 1)
     for two in (0,) + near:
@@ -329,9 +334,7 @@
         + per((3, 4, 4), BF16)
         + per((4, 4), F32)
         + per((4, 4), BF16)
-        + per((3, 4), BF16)
-        + per((4,), F32)
-        + per((3,), F32)
+        + per((15,), BF16)
         + [
             pltpu.VMEM((128, 128), F32),
             dma((8,)),

time: 57.3 us -> 54.1 us (0.944)
  Pallas kernels: 56.5 us -> 53.3 us
    pallas_call x1, Pallas kernels: 53.6 us -> 50.4 us  [step(): pl.pallas_call(step_kernel, out_shape=[pltpu.VMEM((4, 4, 4, 2, t, 8, 128)...]
where the time goes in v5:
time: 54.1 us; the launch traced here: 54 us
  Pallas kernels  53.3 us (99%)
  between operations  0.65 us (1%)
    pallas_call x1, Pallas kernels, step(): pl.pallas_call(step_kernel, out_shape=[pltpu.VMEM((4, 4, 4, 2, t, 8, 128)...  50.4 us
    pallas_call x1, Pallas kernels, finish(): pl.pallas_call(finish_kernel, out_shape=[jax.ShapeDtypeStruct((128, 5, 8,...  2.94 us

profile of v5, /device:TPU:1, one launch (start us, length us, event | category | flops | bytes accessed | tf_op | source)
XLA Modules:
  0.0 54.0 jit_solution(17369158747647986818)
XLA Ops:
  0.6 50.4 %step.1 = (bf16[4,4,4,2,3,8,128]{6,5,4,3,2,1,0:T(8,128)(2,1)S(1)}, bf16[4,4,4,2,4,8,128]{6,5,4,3,2,1,0:T(8,128)(2,1)S(1)}, bf16[4,4,4,2,3,8,128]{6,5,4,3,2,1,0:T...) custom-call(bf16[1024,5120]{1,0:T(8,128)(2,1)} %refs_0_.1, f32[1,5120]{1,0:T(1,128)} %bitcast.33, ...), custom_call_target="tpu_custom_call" | custom-call | flops 2684354560 | bytes 20971520 | tf_op jit(solution)/shard_map/step/pallas_call | solution.py:315
  51.0 2.9 %finish.1 = (bf16[128,5,8,128]{3,2,1,0:T(8,128)(2,1)}, bf16[128,5120]{1,0:T(8,128)(2,1)}, f32[5,8,128]{2,1,0:T(8,128)}, f32[5,8,128]{2,1,0:T(8,128)}, f32[5,8,12...) custom-call(bf16[128,3,8,128]{3,2,1,0:T(8,128)(2,1)S(1)} %bitcast.31, ...), custom_call_target="tpu_custom_call" | custom-call | tf_op jit(solution)/shard_map/finish/pallas_call | solution.py:402
